TPU v7x, 32 devices: a whole 2x2x4 slice. The times are simulated.
32 devices in a mesh: groups: 2 (over x), ep: 8 (over z, y), section: 2 (over core).
Axes of the slice: x: 2, y: 2, z: 4, core: 2. Of those that a mesh axis runs over, the one named last changes fastest.
Arguments:
- resid: bfloat16 [2048, 4096], P(('groups', 'ep')), parts along dimension 0, may hold values from -6 to 6
- norm_gain: bfloat16 [4096], replicated, may hold values from 0.3984375 to 1.59375
- gate_logits: float32 [2048, 8], P(('groups', 'ep')), parts along dimension 0, may hold values from 0.1 to 1
- routes: int32 [2048, 8], P(('groups', 'ep')), parts along dimension 0, may hold values from 0 to 31, all different within a row; in each aligned block of 128 rows (0 to 127, 128 to 255, ...) at most 40 rows name the same one
- w_gate: bfloat16 [32, 4096, 768], P('ep', None, 'section'), may hold values from -0.09375 to 0.09375
- w_up: bfloat16 [32, 4096, 768], P('ep', None, 'section'), may hold values from -0.09375 to 0.09375
- w_down: bfloat16 [32, 768, 4096], P('ep', 'section'), may hold values from -0.21875 to 0.21875
- keys_raw: bfloat16 [2048, 512], P(('groups', 'ep'), 'section'), parts along dimension 0, may hold values from -6 to 6
- values_raw: bfloat16 [2048, 512], P(('groups', 'ep'), 'section'), parts along dimension 0, may hold values from -6 to 6
- k_gain: bfloat16 [128], replicated, may hold values from 0.25 to 1.75
- lengths: int32 [16], P(('groups', 'ep')), parts along dimension 0, may hold values from 32 to 128
- page_owner: int32 [16, 8], P(('groups', 'ep')), parts along dimension 0, may hold values from 0 to 7, as said below
- page_slot: int32 [16, 8], P(('groups', 'ep')), parts along dimension 0, may hold values from 0 to 7, as said below
Outputs:
- moe_out: bfloat16 [2048, 4096], P(('groups', 'ep'), 'section'), parts along dimension 0
- kv_cache: bfloat16 [128, 16, 2, 512], P(('groups', 'ep'), None, None, 'section'), parts along dimension 0
There are 2 independent parts, one for each index of `groups`. A program takes and returns all parts, laid end to end along the dimension named above; an argument that names none is the same for every part. Nothing has to cross between parts.
Inputs may be any that keep to these rules, and one draw needn't show every extreme that they name: `page_owner`: each prompt sends its 8 pages to 4 different owners, exactly 2 pages to each of them; every owner receives exactly 8 pages. `page_slot`: the pages that reach one owner have different slots, so every slot of every owner is filled once.
All inputs are finite; a program needn't handle non-finite values.
Results may differ from a plain program's by a relative error of at most 0.0076.
Values may be sent and summed in bfloat16 or wider, within the bound.
No kernel may reach another device: no remote copies, remote signals or barrier semaphores. Data moves between devices by JAX's collectives and lax.ppermute only.
A program may use at most 128 MiB of HBM per device.

v0:
```python
import functools
import math

import jax
import jax.numpy as jnp
from jax import lax
from jax.experimental import pallas as pl
from jax.experimental.pallas import tpu as pltpu
from jax.sharding import PartitionSpec as P


CAP = 40
PAGE_PEER = 2
LANES = 128
TILE = 160
PARTS = 2
GATE_LIMIT = 48 * 1024 * 1024
DOWN_LIMIT = 24 * 1024 * 1024
SMALL_LIMIT = 12 * 1024 * 1024


def rms_scale(values, gain_row):
    mean_square = jnp.mean(values * values, axis=-1, keepdims=True)
    return values * lax.rsqrt(mean_square + 1e-06) * gain_row


def rotate_keys(key_block, position):
    half_size = key_block.shape[-1] // 2
    frequency = jnp.exp(
        jnp.arange(half_size, dtype=jnp.float32)
        * (-2.0 / key_block.shape[-1])
        * math.log(1000000.0)
    )
    angles = position.astype(jnp.float32)[:, None, None] * frequency
    cosine = jnp.cos(angles)
    sine_part = jnp.sin(angles)
    first_half = key_block[..., :half_size]
    second = key_block[..., half_size:]
    return jnp.concatenate(
        [first_half * cosine - second * sine_part, second * cosine + first_half * sine_part],
        axis=-1,
    )


class Ring:
    def __init__(self, count):
        order = list(range(0, count, 2)) + list(range(1, count, 2))[::-1]
        self.count = count
        self.half = count // 2
        self.up = [(order[i], order[(i + 1) % count]) for i in range(count)]
        self.down = [(b, a) for a, b in self.up]

    def clockwise(self, block):
        return lax.ppermute(block, "ep", self.up)

    def counter(self, block):
        return lax.ppermute(block, "ep", self.down)


def swap_section(block):
    return lax.ppermute(block, "section", [(0, 1), (1, 0)])


def prep_kernel(lengths, resid, gain, logits, routes, out, table):
    rows, width = out.shape[0], resid.shape[1]
    tok_rows = resid.shape[0]
    start = pl.multiple_of(lax.axis_index("section") * rows, rows)
    weights = logits[...]
    weights = weights / jnp.sum(weights, axis=0, keepdims=True)
    weights = weights.astype(jnp.bfloat16).astype(jnp.float32)
    chosen = routes[...]
    expert = lax.broadcasted_iota(jnp.int32, (LANES, tok_rows), 0)
    position = lax.broadcasted_iota(jnp.int32, (LANES, tok_rows), 1)
    mixed = jnp.zeros((LANES, tok_rows), jnp.float32)
    for k in range(chosen.shape[0]):
        mixed = mixed + jnp.where(expert == chosen[k : k + 1, :], weights[k : k + 1, :], 0.0)
    table[...] = jnp.where(position < lengths[0], mixed, 0.0).T
    out[:, width:] = table[pl.ds(start, rows), :].astype(jnp.bfloat16)
    values = resid[pl.ds(start, rows), :].astype(jnp.float32)
    mean_square = jnp.sum(values * values, axis=-1, keepdims=True) * (1.0 / width)
    gains = gain[...].astype(jnp.float32)
    gains = jnp.concatenate([gains[i : i + 1, :] for i in range(width // LANES)], axis=1)
    scaled = values * lax.rsqrt(mean_square + 1e-06) * gains
    out[:, :width] = scaled.astype(jnp.bfloat16)


def prep(lengths, resid, gain, logits, routes):
    tok_rows, width = resid.shape
    whole = pl.BlockSpec(memory_space=pltpu.VMEM)
    return pl.pallas_call(
        prep_kernel,
        out_shape=jax.ShapeDtypeStruct((tok_rows // 2, width + LANES), jnp.bfloat16),
        in_specs=[pl.BlockSpec(memory_space=pltpu.SMEM)] + [whole] * 4,
        out_specs=whole,
        scratch_shapes=[pltpu.VMEM((tok_rows, LANES), jnp.float32)],
        name="prep",
    )(lengths, resid, gain.reshape(width // LANES, LANES), logits.T, routes.T)


def gate_kernel(peer, *refs, count, tokens, width, local, levels):
    blocks = refs[:count]
    w_gate, w_up = refs[count : count + 2]
    active, spread, hold, gates, ups, picked, slot_t, block_sems, weight_sems = refs[-9:]
    copies = []
    start = 0
    for i, block in enumerate(blocks):
        rows = block.shape[0]
        copy = pltpu.make_async_copy(block, hold.at[pl.ds(start, rows), :], block_sems.at[i])
        copy.start()
        copies.append(copy)
        start += rows

    def weights(e):
        return (
            pltpu.make_async_copy(w_gate.at[e], gates.at[e], weight_sems.at[0, e]),
            pltpu.make_async_copy(w_up.at[e], ups.at[e], weight_sems.at[1, e]),
        )

    for copy in weights(0):
        copy.start()
    for copy in copies:
        copy.wait()
    if local > 1:
        for copy in weights(1):
            copy.start()

    lane_in = lax.broadcasted_iota(jnp.int32, (LANES, LANES), 0)
    lane_out = lax.broadcasted_iota(jnp.int32, (LANES, LANES), 1)
    pick = ((lane_in == peer[0] * local + lane_out) & (lane_out < local)).astype(jnp.bfloat16)
    earlier = (lane_out < lane_in).astype(jnp.bfloat16)
    carry = jnp.zeros((1, LANES), jnp.float32)
    capacity = levels * TILE
    column = lax.broadcasted_iota(jnp.int32, (LANES, capacity), 1).astype(jnp.float32)
    for b in range(tokens // LANES):
        span = slice(b * LANES, (b + 1) * LANES)
        mix = jnp.dot(hold[span, width:], pick, preferred_element_type=jnp.float32)
        hit = (mix > 0.0).astype(jnp.float32)
        rank = jnp.dot(earlier, hit.astype(jnp.bfloat16), preferred_element_type=jnp.float32)
        slot = jnp.where(mix > 0.0, rank + carry, -1.0)
        carry = carry + jnp.sum(hit, axis=0, keepdims=True)
        slot_t[:, span] = slot.T[: slot_t.shape[0], :]
        pieces = [
            jnp.where(slot[:, e : e + 1] == column, mix[:, e : e + 1], 0.0) for e in range(local)
        ]
        spread[span, :] = jnp.concatenate(pieces, axis=1).astype(jnp.bfloat16)

    def tile(level, e):
        row = lax.broadcasted_iota(jnp.int32, (TILE, tokens), 0) + level * TILE
        select = (slot_t[pl.ds(e, 1), :] == row.astype(jnp.float32)).astype(jnp.bfloat16)
        step = min(width, 1024)
        for k in range(width // step):
            span = slice(k * step, (k + 1) * step)
            picked[:, span] = jnp.dot(
                select, hold[:, span], preferred_element_type=jnp.float32
            ).astype(jnp.bfloat16)
        gate = jnp.dot(picked[...], gates[e], preferred_element_type=jnp.float32)
        up = jnp.dot(picked[...], ups[e], preferred_element_type=jnp.float32)
        value = gate / (1.0 + jnp.exp(-gate)) * up
        active[e, pl.ds(pl.multiple_of(level * TILE, 32), TILE), :] = value.astype(jnp.bfloat16)

    def expert(e, _):
        for copy in weights(e):
            copy.wait()

        @pl.when(e + 2 < local)
        def _():
            for copy in weights(e + 2):
                copy.start()

        if levels == 1:
            tile(0, e)
        else:
            lax.fori_loop(0, levels, lambda level, _: (tile(level, e), 0)[1], 0)
        return 0

    lax.fori_loop(0, local, expert, 0)


def gate_up(peer, blocks, w_gate, w_up, levels, after=()):
    local, width, units = w_gate.shape
    tokens = sum(block.shape[0] for block in blocks)
    hbm = pl.BlockSpec(memory_space=pl.ANY)
    vmem = pl.BlockSpec(memory_space=pltpu.VMEM)
    smem = pl.BlockSpec(memory_space=pltpu.SMEM)
    return pl.pallas_call(
        functools.partial(
            gate_kernel,
            count=len(blocks),
            tokens=tokens,
            width=width,
            local=local,
            levels=levels,
        ),
        in_specs=[smem] + [hbm] * (len(blocks) + 2 + len(after)),
        out_specs=[vmem, vmem],
        scratch_shapes=[
            pltpu.VMEM((tokens, width + LANES), jnp.bfloat16),
            pltpu.VMEM((local, width, units), jnp.bfloat16),
            pltpu.VMEM((local, width, units), jnp.bfloat16),
            pltpu.VMEM((TILE, width), jnp.bfloat16),
            pltpu.VMEM((max(8, local), tokens), jnp.float32),
            pltpu.SemaphoreType.DMA((len(blocks),)),
            pltpu.SemaphoreType.DMA((2, local)),
        ],
        out_shape=[
            jax.ShapeDtypeStruct((local, levels * TILE, units), jnp.bfloat16),
            jax.ShapeDtypeStruct((tokens, local * levels * TILE), jnp.bfloat16),
        ],
        compiler_params=pltpu.CompilerParams(vmem_limit_bytes=GATE_LIMIT),
        cost_estimate=pl.CostEstimate(
            flops=8_000_000_000, bytes_accessed=4 * local * width * units, transcendentals=0
        ),
        name="gate_up",
    )(peer, *blocks, w_gate, w_up, *after)


def down_kernel(half, active, spread, w_down, *rest):
    out, held = rest[-2:]
    local, capacity, _ = active.shape
    for e in range(local):
        held[e * capacity : (e + 1) * capacity, :] = jnp.dot(
            active[e], w_down[e], preferred_element_type=jnp.float32
        ).astype(jnp.bfloat16)
    out[...] = jnp.dot(spread[...], held[...], preferred_element_type=jnp.float32).astype(out.dtype)


def down_mix(half, active, spread, w_down, columns, dtype, after=(), step=512):
    local, capacity, units = active.shape
    tokens = spread.shape[0]
    steps = columns // step
    keep = lambda *shape: pl.BlockSpec(shape, lambda n, *_: (0,) * len(shape))
    return pl.pallas_call(
        down_kernel,
        grid_spec=pltpu.PrefetchScalarGridSpec(
            num_scalar_prefetch=1,
            grid=(steps,),
            in_specs=[
                keep(local, capacity, units),
                keep(tokens, local * capacity),
                pl.BlockSpec((local, units, step), lambda n, h: (0, 0, h[0] * steps + n)),
            ]
            + [pl.BlockSpec(memory_space=pl.ANY)] * len(after),
            out_specs=pl.BlockSpec((tokens, step), lambda n, h: (0, n)),
            scratch_shapes=[pltpu.VMEM((local * capacity, step), jnp.bfloat16)],
        ),
        out_shape=jax.ShapeDtypeStruct((tokens, columns), dtype),
        compiler_params=pltpu.CompilerParams(
            dimension_semantics=("arbitrary",), vmem_limit_bytes=DOWN_LIMIT
        ),
        cost_estimate=pl.CostEstimate(
            flops=3_000_000_000, bytes_accessed=2 * local * units * columns, transcendentals=0
        ),
        name="down_mix",
    )(half, active, spread, w_down, *after)


def gather_ring(ring, block):
    rows = block.shape[0] // 2
    behind, ahead = [block], [block]
    found = [[block]]
    for _ in range(1, ring.half):
        behind.append(ring.clockwise(behind[-1]))
        ahead.append(ring.counter(ahead[-1]))
        found += [[behind[-1]], [ahead[-1]]]
    far_up = ring.clockwise(behind[-1][:rows])
    far_down = ring.counter(ahead[-1][rows:])
    found.append([far_up, far_down])
    return found


def hop_kernel(*refs, plan):
    outs = refs[-len(plan) :]
    at = 0
    for out, (sides, held) in zip(outs, plan):
        rows = out.shape[0] // len(sides)
        count = len(sides)
        for i, side in enumerate(sides):
            value = refs[at + i][...].astype(jnp.float32)
            value = value + refs[at + count + i][...].astype(jnp.float32)
            if side in held:
                start = held.index(side) * rows
                acc = refs[at + 2 * count]
                value = value + acc[start : start + rows, :].astype(jnp.float32)
            out[i * rows : (i + 1) * rows, :] = value.astype(out.dtype)
        at += 2 * count + (1 if held else 0)


def hop_add(ways, count, column, rows, width):
    operands, specs, plan, shapes = [], [], [], []
    whole = lambda array: pl.BlockSpec(array.shape, lambda _: (0, 0))

    def view(side, place):
        return pl.BlockSpec((rows, width), lambda _: (side * count + place, column))

    for kept, taken, place, sides, acc, held in ways:
        operands += [kept] * len(sides) + [taken] * len(sides)
        specs += [view(side, place) for side in sides] + [view(1 - side, place) for side in sides]
        if held:
            operands.append(acc)
            specs.append(whole(acc))
        plan.append((sides, held))
        shapes.append(jax.ShapeDtypeStruct((len(sides) * rows, width), jnp.bfloat16))
    return pl.pallas_call(
        functools.partial(hop_kernel, plan=tuple(plan)),
        grid=(1,),
        in_specs=specs,
        out_specs=[whole(shape) for shape in shapes],
        out_shape=shapes,
        compiler_params=pltpu.CompilerParams(vmem_limit_bytes=SMALL_LIMIT),
        cost_estimate=pl.CostEstimate(
            flops=1_000_000_000, bytes_accessed=40 * rows * width, transcendentals=0
        ),
        name="hop_add",
    )(*operands)


def last_kernel(kept_0, kept_1, taken_0, taken_1, *refs):
    out = refs[-1]
    rows = kept_0.shape[0]
    width = refs[0].shape[1]
    section = lax.axis_index("section")
    for side, (kept, taken) in enumerate(((kept_0, taken_0), (kept_1, taken_1))):
        start = pl.multiple_of((side + section) % 2 * rows, rows)
        for column in range(len(refs) // 2):
            cols = slice(column * width, (column + 1) * width)
            value = kept[:, cols] + taken[:, cols].astype(jnp.float32)
            for acc in refs[2 * column : 2 * column + 2]:
                value = value + acc[side * rows : (side + 1) * rows, :].astype(jnp.float32)
            out[pl.ds(start, rows), cols] = value.astype(out.dtype)


def last_add(kept, taken, count, rows, arrived):
    total = kept.shape[1]
    view = lambda side: pl.BlockSpec((rows, total), lambda _: (side * count, 0))
    return pl.pallas_call(
        last_kernel,
        grid=(1,),
        in_specs=[view(0), view(1), view(1), view(0)]
        + [pl.BlockSpec(acc.shape, lambda _: (0, 0)) for acc in arrived],
        out_specs=pl.BlockSpec((2 * rows, total), lambda _: (0, 0)),
        out_shape=jax.ShapeDtypeStruct((2 * rows, total), jnp.bfloat16),
        compiler_params=pltpu.CompilerParams(vmem_limit_bytes=SMALL_LIMIT),
        name="last_add",
    )(kept, kept, taken, taken, *arrived)


def scatter_ring(ring, sums, rows, parts):
    count = ring.count // 2
    width = sums[0][0].shape[1] // parts

    moving = [[None, None] for _ in range(parts)]
    for hop in range(ring.half):
        for column in range(parts):
            ways = []
            for way in range(2):
                index = ring.count - 1 if hop == 0 else 2 * (ring.half - hop) - way
                sides = (way,) if hop == 0 else (0, 1)
                held = ((), (way,), (0, 1))[min(hop, 2)]
                kept, taken = sums[index // count]
                ways.append((kept, taken, index % count, sides, moving[column][way], held))
            blocks = hop_add(ways, count, column, rows, width)
            for way, move in enumerate((ring.clockwise, ring.counter)):
                moving[column][way] = move(blocks[way])
    arrived = [acc for pair in moving for acc in pair]
    return last_add(*sums[0], count, rows, arrived)


def kv_part(keys_raw, values_raw, k_gain, is_live, position, page_owner, page_slot):
    tok_rows, kv_width = keys_raw.shape
    head = k_gain.shape[0]
    pages = page_owner.shape[1]
    page = tok_rows // pages
    peer_count = lax.axis_size("ep")
    normed = rms_scale(
        keys_raw.astype(jnp.float32).reshape(tok_rows, kv_width // head, head),
        k_gain.astype(jnp.float32),
    )
    turned = rotate_keys(normed, position)
    key_rows = (
        jnp.where(is_live[:, None, None], turned, 0.0)
        .astype(jnp.bfloat16)
        .reshape(tok_rows, kv_width)
    )
    value_rows = jnp.where(is_live[:, None], values_raw, jnp.zeros_like(values_raw))
    page_rows = jnp.stack([key_rows, value_rows], axis=1).reshape(pages, page * 2 * kv_width)
    owners = page_owner.reshape(-1)
    same = (owners[:, None] == owners[None, :]) & (
        jnp.arange(pages)[None, :] < jnp.arange(pages)[:, None]
    )
    page_rank = jnp.sum(same.astype(jnp.int32), axis=1)
    lane_index = owners * PAGE_PEER + page_rank
    lane_ids = jnp.arange(peer_count * PAGE_PEER, dtype=jnp.int32)
    select = lane_ids[:, None] == lane_index[None, :]
    tagged = jnp.concatenate(
        [
            page_rows,
            jnp.broadcast_to(
                (page_slot.reshape(-1, 1) + 1).astype(jnp.bfloat16), (pages, LANES)
            ),
        ],
        axis=1,
    )
    sent = jnp.dot(
        select.astype(jnp.bfloat16), tagged, preferred_element_type=jnp.float32
    ).astype(jnp.bfloat16)
    sent = sent.reshape(peer_count, PAGE_PEER, tagged.shape[1])
    got = lax.all_to_all(sent, "ep", split_axis=0, concat_axis=0, tiled=True)
    got = got.reshape(peer_count * PAGE_PEER, tagged.shape[1])
    slots = got[:, -1].astype(jnp.int32) - 1
    placing = (jnp.arange(pages, dtype=jnp.int32)[:, None] == slots[None, :]).astype(jnp.bfloat16)
    cache = jnp.dot(placing, got[:, :-LANES], preferred_element_type=jnp.float32)
    return cache.astype(jnp.bfloat16).reshape(pages, page, 2, kv_width)


def shards(
    resid,
    norm_gain,
    gate_logits,
    routes,
    w_gate,
    w_up,
    w_down,
    keys_raw,
    values_raw,
    k_gain,
    lengths,
    page_owner,
    page_slot,
):
    tok_rows, model_width = resid.shape
    section_count = lax.axis_size("section")
    peer_count = lax.axis_size("ep")
    section = lax.axis_index("section")
    peer = lax.axis_index("ep").reshape(1).astype(jnp.int32)
    col_width = model_width // section_count
    ring = Ring(peer_count)
    position = jnp.arange(tok_rows, dtype=jnp.int32)
    is_live = position < lengths[0]

    kv_cache = kv_part(keys_raw, values_raw, k_gain, is_live, position, page_owner, page_slot)

    mine = section.reshape(1).astype(jnp.int32)
    near_count = peer_count // 2
    levels = -(-near_count * CAP // TILE)
    rows = tok_rows // section_count
    payload = prep(lengths, resid, norm_gain, gate_logits, routes)
    found = gather_ring(ring, payload)
    swapped = [[swap_section(piece) for piece in pieces] for pieces in found]
    groups = []
    for span in (slice(0, near_count), slice(near_count, peer_count)):
        blocks = [piece for pieces in found[span] + swapped[span] for piece in pieces]
        after = groups[-1][:1] if groups else ()
        groups.append(gate_up(peer, blocks, w_gate, w_up, levels, after))
    sums = [None, None]
    after = ()
    for group in (0, 1):
        active, spread = groups[group]
        given = down_mix(1 - mine, active, spread, w_down, col_width, jnp.bfloat16, after)
        taken = swap_section(given)
        kept = down_mix(mine, active, spread, w_down, col_width, jnp.float32, (given,))
        sums[group] = (kept, taken)
        after = (kept,)

    return (scatter_ring(ring, sums, rows, PARTS), kv_cache)


def solution(mesh):
    in_specs = (
        P(("groups", "ep"), None),
        P(),
        P(("groups", "ep"), None),
        P(("groups", "ep"), None),
        P("ep", None, "section"),
        P("ep", None, "section"),
        P("ep", "section", None),
        P(("groups", "ep"), "section"),
        P(("groups", "ep"), "section"),
        P(),
        P(("groups", "ep")),
        P(("groups", "ep"), None),
        P(("groups", "ep"), None),
    )
    out_specs = (P(("groups", "ep"), "section"), P(("groups", "ep"), None, None, "section"))

    return jax.shard_map(shards, mesh=mesh, in_specs=in_specs, out_specs=out_specs, check_vma=False)
```

profile of v0, /device:TPU:0, one launch (start us, length us, event | category | flops | bytes accessed | tf_op | source)
XLA Modules:
  0.0 181.0 jit_solution(3169055274420868826)
XLA Ops:
  1.3 2.4 %prep.1.refs_0_ = bf16[64,4224]{1,0:T(8,128)(2,1)} custom-call(s32[1]{0:T(128)} %copy.31.lengths, bf16[128,4096]{1,0:T(8,128)(2,1)} %resid.1, bf16[32,128]{1,0:T(8,128)(2,1)} %bitcast.20, f32[8,128]{1,0:T(8,128)} %bitcast.21, s32[8,128]{1,0:T(8,128)} %bitcast.22), custom_call_target="tpu_custom_call" | custom-call | tf_op jit(solution)/shard_map/prep/pallas_call | solution.py:90
  3.7 3.1 %collective-permute-start = (bf16[64,4224]{1,0:T(8,128)(2,1)}, bf16[64,4224]{1,0:T(8,128)(2,1)S(1)}, u32[]{:S(2)}, u32[]{:S(2)}) collective-permute-start(bf16[64,4224]{1,0:T(8,128)(2,1)} %prep.1.refs_0_), channel_id=1, source_target_pairs={{0,4},{4,8},{8,12},{12,14},{14,10},{10,6},{6,2},{2,0},{1,5},{5,9},... | collective-permute-start | bytes 1622024 | tf_op jit(solution)/shard_map/ppermute | solution.py:54
  6.7 12.4 %collective-permute-done.refs_1_ = bf16[64,4224]{1,0:T(8,128)(2,1)S(1)} collective-permute-done((bf16[64,4224]{1,0:T(8,128)(2,1)}, bf16[64,4224]{1,0:T(8,128)(2,1)S(1)}, u32[]{:S(2)}, u32[]{:S(2)}) %collective-permute-start) | collective-permute-done | bytes 540704 | tf_op jit(solution)/shard_map/ppermute | solution.py:54
  21.2 11.4 %collective-permute-done.2.refs_3_ = bf16[64,4224]{1,0:T(8,128)(2,1)S(1)} collective-permute-done((bf16[64,4224]{1,0:T(8,128)(2,1)S(1)}, bf16[64,4224]{1,0:T(8,128)(2,1)S(1)}, u32[]{:S(2)}, u32[]{:S(2)}) %collective-permute-start.2) | collective-permute-done | bytes 540704 | tf_op jit(solution)/shard_map/ppermute | solution.py:54
  36.1 9.1 %collective-permute-done.9.refs_1_ = bf16[64,4224]{1,0:T(8,128)(2,1)S(1)} collective-permute-done((bf16[64,4224]{1,0:T(8,128)(2,1)S(1)}, bf16[64,4224]{1,0:T(8,128)(2,1)S(1)}, u32[]{:S(2)}, u32[]{:S(2)}) %collective-permute-start.9) | collective-permute-done | bytes 540704 | tf_op jit(solution)/shard_map/ppermute | solution.py:54
  46.9 10.0 %collective-permute-done.10.refs_2_ = bf16[64,4224]{1,0:T(8,128)(2,1)S(1)} collective-permute-done((bf16[64,4224]{1,0:T(8,128)(2,1)S(1)}, bf16[64,4224]{1,0:T(8,128)(2,1)S(1)}, u32[]{:S(2)}, u32[]{:S(2)}) %collective-permute-start.10) | collective-permute-done | bytes 540704 | tf_op jit(solution)/shard_map/ppermute | solution.py:57
  60.6 12.3 %gate_up.2 = (bf16[4,160,384]{2,1,0:T(8,128)(2,1)S(1)}, bf16[512,640]{1,0:T(8,128)(2,1)S(1)}) custom-call(s32[1]{0:T(128)} %bitcast.1.peer, bf16[64,4224]{1,0:T(8,128)(2,1)S(1)} %copy-done.11, bf16[64,4224]{1,0:T(8,128)(2,1)S(1)} %collective-permute-done.refs_1_, bf16[64,4224]{1,0:T(8,128)(2,1)S(1)} %collective-permute-done.1.refs_2_, ...), custom_call_target="tpu_custom_call" | custom-call | flops 8000000000 | bytes 25165824 | tf_op jit(solution)/shard_map/gate_up/pallas_call | solution.py:185
  72.9 4.6 %copy-done.6 = bf16[4,384,4096]{2,1,0:T(8,128)(2,1)S(1)} copy-done((bf16[4,384,4096]{2,1,0:T(8,128)(2,1)S(1)}, bf16[4,384,4096]{2,1,0:T(8,128)(2,1)}, u32[]{:S(2)}) %copy-start.6) | copy-done | bytes 12582936
  77.5 4.3 %down_mix.4.rest_0_ = bf16[512,2048]{1,0:T(8,128)(2,1)S(1)} custom-call(s32[1]{0:T(128)S(6)} %sub.12.half, bf16[4,160,384]{2,1,0:T(8,128)(2,1)S(1)} %get-tuple-element.22.active.refs_12_, bf16[512,640]{1,0:T(8,128)(2,1)S(1)} %get-tuple-element.23.spread, bf16[4,384,4096]{2,1,0:T(8,128)(2,1)S(1)} %copy-done.6), custom_call_target="tpu_custom_call" | custom-call | flops 3000000000 | bytes 6291456 | tf_op jit(solution)/shard_map/down_mix/pallas_call | solution.py:232
  82.4 4.7 %copy-done.7 = bf16[4,384,4096]{2,1,0:T(8,128)(2,1)S(1)} copy-done((bf16[4,384,4096]{2,1,0:T(8,128)(2,1)S(1)}, bf16[4,384,4096]{2,1,0:T(8,128)(2,1)}, u32[]{:S(2)}) %copy-start.7) | copy-done | bytes 12582936
  87.1 4.4 %down_mix.5.rest_0_.refs_5_.refs_6_.refs_0_.refs_1_.kept_0.kept_1 = f32[512,2048]{1,0:T(8,128)S(1)} custom-call(s32[1]{0:T(128)} %bitcast.half, bf16[4,160,384]{2,1,0:T(8,128)(2,1)S(1)} %get-tuple-element.22.active.refs_12_, bf16[512,640]{1,0:T(8,128)(2,1)S(1)} %get-tuple-element.23.spread, bf16[4,384,4096]{2,1,0:T(8,128)(2,1)S(1)} %copy-done.7, ...), custom_call_target="tpu_custom_call" | custom-call | flops 3000000000 | bytes 6291456 | tf_op jit(solution)/shard_map/down_mix/pallas_call | solution.py:232
  91.6 13.3 %gate_up.3 = (bf16[4,160,384]{2,1,0:T(8,128)(2,1)S(1)}, bf16[512,640]{1,0:T(8,128)(2,1)S(1)}) custom-call(s32[1]{0:T(128)} %bitcast.1.peer, bf16[64,4224]{1,0:T(8,128)(2,1)S(1)} %collective-permute-done.8.refs_0_, bf16[64,4224]{1,0:T(8,128)(2,1)S(1)} %collective-permute-done.9.refs_1_, bf16[64,4224]{1,0:T(8,128)(2,1)S(1)} %collective-permute-done.10.refs_2_, ...), custom_call_target="tpu_custom_call" | custom-call | flops 8000000000 | bytes 25165824 | tf_op jit(solution)/shard_map/gate_up/pallas_call | solution.py:185
  105.0 4.6 %copy-done.8 = bf16[4,384,4096]{2,1,0:T(8,128)(2,1)S(1)} copy-done((bf16[4,384,4096]{2,1,0:T(8,128)(2,1)S(1)}, bf16[4,384,4096]{2,1,0:T(8,128)(2,1)}, u32[]{:S(2)}) %copy-start.8) | copy-done | bytes 12582936
  109.6 5.0 %down_mix.6.rest_0_ = bf16[512,2048]{1,0:T(8,128)(2,1)} custom-call(s32[1]{0:T(128)S(6)} %sub.12.half, bf16[4,160,384]{2,1,0:T(8,128)(2,1)S(1)} %get-tuple-element.24.active, bf16[512,640]{1,0:T(8,128)(2,1)S(1)} %get-tuple-element.25.spread, bf16[4,384,4096]{2,1,0:T(8,128)(2,1)S(1)} %copy-done.8, ...), custom_call_target="tpu_custom_call" | custom-call | flops 3000000000 | bytes 6291456 | tf_op jit(solution)/shard_map/down_mix/pallas_call | solution.py:232
  116.4 4.6 %copy-done.9 = bf16[4,384,4096]{2,1,0:T(8,128)(2,1)S(1)} copy-done((bf16[4,384,4096]{2,1,0:T(8,128)(2,1)S(1)}, bf16[4,384,4096]{2,1,0:T(8,128)(2,1)}, u32[]{:S(2)}) %copy-start.9) | copy-done | bytes 12582936
  121.0 4.4 %down_mix.7.refs_0_.refs_2_.refs_1_.refs_5_.refs_6_ = f32[512,2048]{1,0:T(8,128)S(1)} custom-call(s32[1]{0:T(128)} %bitcast.half, bf16[4,160,384]{2,1,0:T(8,128)(2,1)S(1)} %get-tuple-element.24.active, bf16[512,640]{1,0:T(8,128)(2,1)S(1)} %get-tuple-element.25.spread, bf16[4,384,4096]{2,1,0:T(8,128)(2,1)S(1)} %copy-done.9, bf16[512,2048]{1,0:T(8,128)(2,1)} %down_mix.6.rest_0_), custom_call_target="tpu_custom_call" | custom-call | flops 3000000000 | bytes 6291456 | tf_op jit(solution)/shard_map/down_mix/pallas_call | solution.py:232
  132.5 2.2 %copy-done.1 = f32[512,2048]{1,0:T(8,128)S(1)} copy-done((f32[512,2048]{1,0:T(8,128)S(1)}, f32[512,2048]{1,0:T(8,128)}, u32[]{:S(2)}) %copy-start.1) | copy-done | bytes 4194328
  143.2 4.8 %all-to-all-start = ((bf16[8,2,8320]{2,1,0:T(2,128)(2,1)}), bf16[8,2,8320]{2,1,0:T(2,128)(2,1)}, u32[]{:S(2)}, u32[]{:S(2)}) async-start(bf16[8,2,8320]{2,1,0:T(2,128)(2,1)} %reshape.171), calls=%async_computation | async-start | bytes 532480 | tf_op jit(solution)/shard_map/all_to_all | solution.py:407
  148.0 2.2 %copy-done.2 = f32[512,2048]{1,0:T(8,128)S(1)} copy-done((f32[512,2048]{1,0:T(8,128)S(1)}, f32[512,2048]{1,0:T(8,128)}, u32[]{:S(2)}) %copy-start.2) | copy-done | bytes 4194328
  150.2 2.2 %copy-done.4 = f32[512,2048]{1,0:T(8,128)S(1)} copy-done((f32[512,2048]{1,0:T(8,128)S(1)}, f32[512,2048]{1,0:T(8,128)}, u32[]{:S(2)}) %copy-start.4) | copy-done | bytes 4194328
  154.2 2.0 %collective-permute-start.23 = (bf16[128,1024]{1,0:T(8,128)(2,1)}, bf16[128,1024]{1,0:T(8,128)(2,1)S(1)}, u32[]{:S(2)}, u32[]{:S(2)}) collective-permute-start(bf16[128,1024]{1,0:T(8,128)(2,1)} %get-tuple-element.30), channel_id=1, source_target_pairs={{0,4},{4,8},{8,12},{12,14},{14,10},{10,6},{6,2},{2,0},{1,5},{5,9},... | collective-permute-start | bytes 786440 | tf_op jit(solution)/shard_map/ppermute | solution.py:54
  158.2 2.0 %collective-permute-start.31 = (bf16[128,1024]{1,0:T(8,128)(2,1)}, bf16[128,1024]{1,0:T(8,128)(2,1)S(1)}, u32[]{:S(2)}, u32[]{:S(2)}) collective-permute-start(bf16[128,1024]{1,0:T(8,128)(2,1)} %get-tuple-element.38), channel_id=1, source_target_pairs={{0,4},{4,8},{8,12},{12,14},{14,10},{10,6},{6,2},{2,0},{1,5},{5,9},... | collective-permute-start | bytes 786440 | tf_op jit(solution)/shard_map/ppermute | solution.py:54
  164.2 2.2 %copy-done.5 = f32[512,2048]{1,0:T(8,128)S(1)} copy-done((f32[512,2048]{1,0:T(8,128)S(1)}, f32[512,2048]{1,0:T(8,128)}, u32[]{:S(2)}) %copy-start.5) | copy-done | bytes 4194328
  178.9 2.1 %last_add.1 = bf16[128,2048]{1,0:T(8,128)(2,1)} custom-call(f32[512,2048]{1,0:T(8,128)S(1)} %copy-done.5, f32[512,2048]{1,0:T(8,128)S(1)} %copy-done.5, bf16[512,2048]{1,0:T(8,128)(2,1)} %collective-permute-done.7.refs_7_.refs_8_.refs_2_.refs_3_.taken_0.taken_1, bf16[512,2048]{1,0:T(8,128)(2,1)} %collective-permute-done.7.refs_7_.refs_8_.refs_2_.refs_3_.taken_0.taken_1, ...), custom_call_target="tpu_custom_call" | custom-call | tf_op jit(solution)/shard_map/last_add/pallas_call | solution.py:335
  (129 shorter events, 49.1 us)
Async XLA Ops:
  3.7 15.5 %collective-permute-start = (bf16[64,4224]{1,0:T(8,128)(2,1)}, bf16[64,4224]{1,0:T(8,128)(2,1)S(1)}, u32[]{:S(2)}, u32[]{:S(2)}) collective-permute-start(bf16[64,4224]{1,0:T(8,128)(2,1)} %prep.1.refs_0_), channel_id=1, source_target_pairs={{0,4},{4,8},{8,12},{12,14},{14,10},{10,6},{6,2},{2,0},{1,5},{5,9},... | collective-permute-start | bytes 1622024 | tf_op jit(solution)/shard_map/ppermute | solution.py:54
  6.7 14.2 %collective-permute-start.1 = (bf16[64,4224]{1,0:T(8,128)(2,1)}, bf16[64,4224]{1,0:T(8,128)(2,1)S(1)}, u32[]{:S(2)}, u32[]{:S(2)}) collective-permute-start(bf16[64,4224]{1,0:T(8,128)(2,1)} %prep.1.refs_0_), channel_id=1, source_target_pairs={{4,0},{8,4},{12,8},{14,12},{10,14},{6,10},{2,6},{0,2},{5,1},{9,5},... | collective-permute-start | bytes 1622024 | tf_op jit(solution)/shard_map/ppermute | solution.py:57
  19.2 13.4 %collective-permute-start.2 = (bf16[64,4224]{1,0:T(8,128)(2,1)S(1)}, bf16[64,4224]{1,0:T(8,128)(2,1)S(1)}, u32[]{:S(2)}, u32[]{:S(2)}) collective-permute-start(bf16[64,4224]{1,0:T(8,128)(2,1)S(1)} %collective-permute-done.refs_1_), channel_id=1, source_target_pairs={{0,4},{4,8},{8,12},{12,14},{14,10},{10,6},{6,2},{2,0},{1,5},{5,9},... | collective-permute-start | bytes 1622024 | tf_op jit(solution)/shard_map/ppermute | solution.py:54
  21.0 14.7 %collective-permute-start.8 = (bf16[64,4224]{1,0:T(8,128)(2,1)S(1)}, bf16[64,4224]{1,0:T(8,128)(2,1)S(1)}, u32[]{:S(2)}, u32[]{:S(2)}) collective-permute-start(bf16[64,4224]{1,0:T(8,128)(2,1)S(1)} %collective-permute-done.1.refs_2_), channel_id=1, source_target_pairs={{4,0},{8,4},{12,8},{14,12},{10,14},{6,10},{2,6},{0,2},{5,1},{9,5},... | collective-permute-start | bytes 1622024 | tf_op jit(solution)/shard_map/ppermute | solution.py:57
  32.6 12.6 %collective-permute-start.9 = (bf16[64,4224]{1,0:T(8,128)(2,1)S(1)}, bf16[64,4224]{1,0:T(8,128)(2,1)S(1)}, u32[]{:S(2)}, u32[]{:S(2)}) collective-permute-start(bf16[64,4224]{1,0:T(8,128)(2,1)S(1)} %collective-permute-done.2.refs_3_), channel_id=1, source_target_pairs={{0,4},{4,8},{8,12},{12,14},{14,10},{10,6},{6,2},{2,0},{1,5},{5,9},... | collective-permute-start | bytes 1622024 | tf_op jit(solution)/shard_map/ppermute | solution.py:54
  34.1 22.8 %collective-permute-start.3 = (bf16[64,4224]{1,0:T(8,128)(2,1)}, bf16[64,4224]{1,0:T(8,128)(2,1)}, u32[]{:S(2)}, u32[]{:S(2)}) collective-permute-start(bf16[64,4224]{1,0:T(8,128)(2,1)} %prep.1.refs_0_), channel_id=1, source_target_pairs={{0,1},{1,0},{2,3},{3,2},{4,5},{5,4},{6,7},{7,6},{8,9},{9,8},{10,11... | collective-permute-start | bytes 1622024 | tf_op jit(solution)/shard_map/ppermute | solution.py:61
  35.0 22.9 %collective-permute-start.4 = (bf16[64,4224]{1,0:T(8,128)(2,1)S(1)}, bf16[64,4224]{1,0:T(8,128)(2,1)S(1)}, u32[]{:S(2)}, u32[]{:S(2)}) collective-permute-start(bf16[64,4224]{1,0:T(8,128)(2,1)S(1)} %collective-permute-done.refs_1_), channel_id=1, source_target_pairs={{0,1},{1,0},{2,3},{3,2},{4,5},{5,4},{6,7},{7,6},{8,9},{9,8},{10,11... | collective-permute-start | bytes 1622024 | tf_op jit(solution)/shard_map/ppermute | solution.py:61
  35.6 23.4 %collective-permute-start.5 = (bf16[64,4224]{1,0:T(8,128)(2,1)S(1)}, bf16[64,4224]{1,0:T(8,128)(2,1)S(1)}, u32[]{:S(2)}, u32[]{:S(2)}) collective-permute-start(bf16[64,4224]{1,0:T(8,128)(2,1)S(1)} %collective-permute-done.1.refs_2_), channel_id=1, source_target_pairs={{0,1},{1,0},{2,3},{3,2},{4,5},{5,4},{6,7},{7,6},{8,9},{9,8},{10,11... | collective-permute-start | bytes 1622024 | tf_op jit(solution)/shard_map/ppermute | solution.py:61
  35.7 23.3 %collective-permute-start.6 = (bf16[64,4224]{1,0:T(8,128)(2,1)S(1)}, bf16[64,4224]{1,0:T(8,128)(2,1)S(1)}, u32[]{:S(2)}, u32[]{:S(2)}) collective-permute-start(bf16[64,4224]{1,0:T(8,128)(2,1)S(1)} %collective-permute-done.2.refs_3_), channel_id=1, source_target_pairs={{0,1},{1,0},{2,3},{3,2},{4,5},{5,4},{6,7},{7,6},{8,9},{9,8},{10,11... | collective-permute-start | bytes 1622024 | tf_op jit(solution)/shard_map/ppermute | solution.py:61
  45.2 11.7 %collective-permute-start.10 = (bf16[64,4224]{1,0:T(8,128)(2,1)S(1)}, bf16[64,4224]{1,0:T(8,128)(2,1)S(1)}, u32[]{:S(2)}, u32[]{:S(2)}) collective-permute-start(bf16[64,4224]{1,0:T(8,128)(2,1)S(1)} %collective-permute-done.8.refs_0_), channel_id=1, source_target_pairs={{4,0},{8,4},{12,8},{14,12},{10,14},{6,10},{2,6},{0,2},{5,1},{9,5},... | collective-permute-start | bytes 1622024 | tf_op jit(solution)/shard_map/ppermute | solution.py:57
  56.9 34.7 %collective-permute-start.13 = (bf16[64,4224]{1,0:T(8,128)(2,1)S(1)}, bf16[64,4224]{1,0:T(8,128)(2,1)S(1)}, u32[]{:S(2)}, u32[]{:S(2)}) collective-permute-start(bf16[64,4224]{1,0:T(8,128)(2,1)S(1)} %collective-permute-done.8.refs_0_), channel_id=1, source_target_pairs={{0,1},{1,0},{2,3},{3,2},{4,5},{5,4},{6,7},{7,6},{8,9},{9,8},{10,11... | collective-permute-start | bytes 1622024 | tf_op jit(solution)/shard_map/ppermute | solution.py:61
  56.9 24.9 %collective-permute-start.11 = (bf16[32,4224]{1,0:T(8,128)(2,1)S(1)}, bf16[32,4224]{1,0:T(8,128)(2,1)S(1)}, u32[]{:S(2)}, u32[]{:S(2)}) collective-permute-start(bf16[32,4224]{1,0:T(8,128)(2,1)S(1)} %slice.24), channel_id=1, source_target_pairs={{0,4},{4,8},{8,12},{12,14},{14,10},{10,6},{6,2},{2,0},{1,5},{5,9},... | collective-permute-start | bytes 811016 | tf_op jit(solution)/shard_map/ppermute | solution.py:54
  58.0 24.0 %collective-permute-start.12 = (bf16[32,4224]{1,0:T(8,128)(2,1)S(1)}, bf16[32,4224]{1,0:T(8,128)(2,1)S(1)}, u32[]{:S(2)}, u32[]{:S(2)}) collective-permute-start(bf16[32,4224]{1,0:T(8,128)(2,1)S(1)} %slice.25), channel_id=1, source_target_pairs={{4,0},{8,4},{12,8},{14,12},{10,14},{6,10},{2,6},{0,2},{5,1},{9,5},... | collective-permute-start | bytes 811016 | tf_op jit(solution)/shard_map/ppermute | solution.py:57
  59.0 32.6 %collective-permute-start.14 = (bf16[64,4224]{1,0:T(8,128)(2,1)S(1)}, bf16[64,4224]{1,0:T(8,128)(2,1)S(1)}, u32[]{:S(2)}, u32[]{:S(2)}) collective-permute-start(bf16[64,4224]{1,0:T(8,128)(2,1)S(1)} %collective-permute-done.9.refs_1_), channel_id=1, source_target_pairs={{0,1},{1,0},{2,3},{3,2},{4,5},{5,4},{6,7},{7,6},{8,9},{9,8},{10,11... | collective-permute-start | bytes 1622024 | tf_op jit(solution)/shard_map/ppermute | solution.py:61
  59.0 32.6 %collective-permute-start.15 = (bf16[64,4224]{1,0:T(8,128)(2,1)S(1)}, bf16[64,4224]{1,0:T(8,128)(2,1)S(1)}, u32[]{:S(2)}, u32[]{:S(2)}) collective-permute-start(bf16[64,4224]{1,0:T(8,128)(2,1)S(1)} %collective-permute-done.10.refs_2_), channel_id=1, source_target_pairs={{0,1},{1,0},{2,3},{3,2},{4,5},{5,4},{6,7},{7,6},{8,9},{9,8},{10,11... | collective-permute-start | bytes 1622024 | tf_op jit(solution)/shard_map/ppermute | solution.py:61
  114.6 10.8 %collective-permute-start.18 = (bf16[512,2048]{1,0:T(8,128)(2,1)}, bf16[512,2048]{1,0:T(8,128)(2,1)S(1)}, u32[]{:S(2)}, u32[]{:S(2)}) collective-permute-start(bf16[512,2048]{1,0:T(8,128)(2,1)} %down_mix.6.rest_0_), channel_id=1, source_target_pairs={{0,1},{1,0},{2,3},{3,2},{4,5},{5,4},{6,7},{7,6},{8,9},{9,8},{10,11... | collective-permute-start | bytes 6291464 | tf_op jit(solution)/shard_map/ppermute | solution.py:61
  115.7 32.3 %collective-permute-start.7 = (bf16[512,2048]{1,0:T(8,128)(2,1)}, bf16[512,2048]{1,0:T(8,128)(2,1)}, u32[]{:S(2)}, u32[]{:S(2)}) collective-permute-start(bf16[512,2048]{1,0:T(8,128)(2,1)} %copy-done.10), channel_id=1, source_target_pairs={{0,1},{1,0},{2,3},{3,2},{4,5},{5,4},{6,7},{7,6},{8,9},{9,8},{10,11... | collective-permute-start | bytes 6291464 | tf_op jit(solution)/shard_map/ppermute | solution.py:61
  127.6 9.9 %collective-permute-start.27 = (bf16[64,1024]{1,0:T(8,128)(2,1)S(1)}, bf16[64,1024]{1,0:T(8,128)(2,1)S(1)}, u32[]{:S(2)}, u32[]{:S(2)}) collective-permute-start(bf16[64,1024]{1,0:T(8,128)(2,1)S(1)} %get-tuple-element.34), channel_id=1, source_target_pairs={{0,4},{4,8},{8,12},{12,14},{14,10},{10,6},{6,2},{2,0},{1,5},{5,9},... | collective-permute-start | bytes 393224 | tf_op jit(solution)/shard_map/ppermute | solution.py:54
  135.5 12.5 %collective-permute-start.21 = (bf16[128,1024]{1,0:T(8,128)(2,1)}, bf16[128,1024]{1,0:T(8,128)(2,1)S(1)}, u32[]{:S(2)}, u32[]{:S(2)}) collective-permute-start(bf16[128,1024]{1,0:T(8,128)(2,1)} %get-tuple-element.28), channel_id=1, source_target_pairs={{0,4},{4,8},{8,12},{12,14},{14,10},{10,6},{6,2},{2,0},{1,5},{5,9},... | collective-permute-start | bytes 786440 | tf_op jit(solution)/shard_map/ppermute | solution.py:54
  137.1 10.9 %collective-permute-start.22 = (bf16[128,1024]{1,0:T(8,128)(2,1)S(1)}, bf16[128,1024]{1,0:T(8,128)(2,1)S(1)}, u32[]{:S(2)}, u32[]{:S(2)}) collective-permute-start(bf16[128,1024]{1,0:T(8,128)(2,1)S(1)} %get-tuple-element.29), channel_id=1, source_target_pairs={{4,0},{8,4},{12,8},{14,12},{10,14},{6,10},{2,6},{0,2},{5,1},{9,5},... | collective-permute-start | bytes 786440 | tf_op jit(solution)/shard_map/ppermute | solution.py:57
  138.4 17.8 %collective-permute-start.29 = (bf16[128,1024]{1,0:T(8,128)(2,1)}, bf16[128,1024]{1,0:T(8,128)(2,1)S(1)}, u32[]{:S(2)}, u32[]{:S(2)}) collective-permute-start(bf16[128,1024]{1,0:T(8,128)(2,1)} %get-tuple-element.36), channel_id=1, source_target_pairs={{0,4},{4,8},{8,12},{12,14},{14,10},{10,6},{6,2},{2,0},{1,5},{5,9},... | collective-permute-start | bytes 786440 | tf_op jit(solution)/shard_map/ppermute | solution.py:54
  140.0 16.3 %collective-permute-start.30 = (bf16[128,1024]{1,0:T(8,128)(2,1)}, bf16[128,1024]{1,0:T(8,128)(2,1)S(1)}, u32[]{:S(2)}, u32[]{:S(2)}) collective-permute-start(bf16[128,1024]{1,0:T(8,128)(2,1)} %get-tuple-element.37), channel_id=1, source_target_pairs={{4,0},{8,4},{12,8},{14,12},{10,14},{6,10},{2,6},{0,2},{5,1},{9,5},... | collective-permute-start | bytes 786440 | tf_op jit(solution)/shard_map/ppermute | solution.py:57
  143.2 17.0 %all-to-all-start = ((bf16[8,2,8320]{2,1,0:T(2,128)(2,1)}), bf16[8,2,8320]{2,1,0:T(2,128)(2,1)}, u32[]{:S(2)}, u32[]{:S(2)}) async-start(bf16[8,2,8320]{2,1,0:T(2,128)(2,1)} %reshape.171), calls=%async_computation | async-start | bytes 532480 | tf_op jit(solution)/shard_map/all_to_all | solution.py:407
  158.2 11.6 %collective-permute-start.31 = (bf16[128,1024]{1,0:T(8,128)(2,1)}, bf16[128,1024]{1,0:T(8,128)(2,1)S(1)}, u32[]{:S(2)}, u32[]{:S(2)}) collective-permute-start(bf16[128,1024]{1,0:T(8,128)(2,1)} %get-tuple-element.38), channel_id=1, source_target_pairs={{0,4},{4,8},{8,12},{12,14},{14,10},{10,6},{6,2},{2,0},{1,5},{5,9},... | collective-permute-start | bytes 786440 | tf_op jit(solution)/shard_map/ppermute | solution.py:54
  (30 other events, 198.5 us)
where the time goes:
time: 182 us; the launch traced here: 181 us
  Pallas kernels  56.4 us (31%)
  waiting for transfers between devices  53.1 us (29%)
  starting transfers between devices  33.8 us (19%)
  local copies, waits for them, and re-layouts  33.1 us (18%)
    ppermute x12, waiting for transfers between devices, clockwise(): return lax.ppermute(block, 'ep', self.up)  38.2 us
    unnamed x37, local copies, waits for them, and re-layouts  29 us
    pallas_call x2, Pallas kernels, gate_up(): pl.pallas_call(functools.partial(gate_kernel, count=len(blocks), tokens=t...  25.7 us
    ppermute x12, starting transfers between devices, clockwise(): return lax.ppermute(block, 'ep', self.up)  19.6 us
    pallas_call x4, Pallas kernels, down_mix(): pl.pallas_call(down_kernel, grid_spec=pltpu.PrefetchScalarGridSpec(num_sc...  18.2 us
    ppermute x12, waiting for transfers between devices, counter(): return lax.ppermute(block, 'ep', self.down)  14.9 us
    pallas_call x8, Pallas kernels, hop_add(): pl.pallas_call(functools.partial(hop_kernel, plan=tuple(plan)), grid=(1,)...  8.05 us
    ppermute x12, starting transfers between devices, counter(): return lax.ppermute(block, 'ep', self.down)  6.67 us
  transfers between devices with their start and end apart: 36, of which 11 were waited for; matrix products, arithmetic and copies ran while one was open for 4% of the time, Pallas kernels for 19%

commit v1 on v0

--- a/solution.py
+++ b/solution.py
@@ -14,8 +14,9 @@
 LANES = 128
 TILE = 160
 PARTS = 2
+SLOTS = 3
 GATE_LIMIT = 48 * 1024 * 1024
-DOWN_LIMIT = 24 * 1024 * 1024
+DOWN_LIMIT = 44 * 1024 * 1024
 SMALL_LIMIT = 12 * 1024 * 1024
 
 
@@ -101,6 +102,7 @@
     blocks = refs[:count]
     w_gate, w_up = refs[count : count + 2]
     active, spread, hold, gates, ups, picked, slot_t, block_sems, weight_sems = refs[-9:]
+    slots = gates.shape[0]
     copies = []
     start = 0
     for i, block in enumerate(blocks):
@@ -112,8 +114,8 @@
 
     def weights(e):
         return (
-            pltpu.make_async_copy(w_gate.at[e], gates.at[e], weight_sems.at[0, e]),
-            pltpu.make_async_copy(w_up.at[e], ups.at[e], weight_sems.at[1, e]),
+            pltpu.make_async_copy(w_gate.at[e], gates.at[e % slots], weight_sems.at[0, e]),
+            pltpu.make_async_copy(w_up.at[e], ups.at[e % slots], weight_sems.at[1, e]),
         )
 
     for copy in weights(0):
@@ -153,8 +155,8 @@
             picked[:, span] = jnp.dot(
                 select, hold[:, span], preferred_element_type=jnp.float32
             ).astype(jnp.bfloat16)
-        gate = jnp.dot(picked[...], gates[e], preferred_element_type=jnp.float32)
-        up = jnp.dot(picked[...], ups[e], preferred_element_type=jnp.float32)
+        gate = jnp.dot(picked[...], gates[e % slots], preferred_element_type=jnp.float32)
+        up = jnp.dot(picked[...], ups[e % slots], preferred_element_type=jnp.float32)
         value = gate / (1.0 + jnp.exp(-gate)) * up
         active[e, pl.ds(pl.multiple_of(level * TILE, 32), TILE), :] = value.astype(jnp.bfloat16)
 
@@ -195,8 +197,8 @@
         out_specs=[vmem, vmem],
         scratch_shapes=[
             pltpu.VMEM((tokens, width + LANES), jnp.bfloat16),
-            pltpu.VMEM((local, width, units), jnp.bfloat16),
-            pltpu.VMEM((local, width, units), jnp.bfloat16),
+            pltpu.VMEM((min(local, SLOTS), width, units), jnp.bfloat16),
+            pltpu.VMEM((min(local, SLOTS), width, units), jnp.bfloat16),
             pltpu.VMEM((TILE, width), jnp.bfloat16),
             pltpu.VMEM((max(8, local), tokens), jnp.float32),
             pltpu.SemaphoreType.DMA((len(blocks),)),
@@ -323,7 +325,7 @@
         start = pl.multiple_of((side + section) % 2 * rows, rows)
         for column in range(len(refs) // 2):
             cols = slice(column * width, (column + 1) * width)
-            value = kept[:, cols] + taken[:, cols].astype(jnp.float32)
+            value = kept[:, cols].astype(jnp.float32) + taken[:, cols].astype(jnp.float32)
             for acc in refs[2 * column : 2 * column + 2]:
                 value = value + acc[side * rows : (side + 1) * rows, :].astype(jnp.float32)
             out[pl.ds(start, rows), cols] = value.astype(out.dtype)
@@ -457,7 +459,7 @@
         active, spread = groups[group]
         given = down_mix(1 - mine, active, spread, w_down, col_width, jnp.bfloat16, after)
         taken = swap_section(given)
-        kept = down_mix(mine, active, spread, w_down, col_width, jnp.float32, (given,))
+        kept = down_mix(mine, active, spread, w_down, col_width, jnp.bfloat16, (given,))
         sums[group] = (kept, taken)
         after = (kept,)
 

time: 182 us -> 168 us (0.923)
  local copies, waits for them, and re-layouts: 33.1 us -> 9.1 us
  Pallas kernels: 56.4 us -> 67 us
    unnamed x37 -> x21, local copies, waits for them, and re-layouts: 29 us -> 5.02 us
    pallas_call x4, Pallas kernels: 18.2 us -> 25.2 us  [down_mix(): pl.pallas_call(down_kernel, grid_spec=pltpu.PrefetchScalarGridSpec(num_sc...]
    pallas_call x8, Pallas kernels: 8.05 us -> 12.4 us  [hop_add(): pl.pallas_call(functools.partial(hop_kernel, plan=tuple(plan)), grid=(1,)...]
  transfers between devices with their start and end apart: 36 -> 36, of which waited for: 11 -> 13; matrix products, arithmetic and copies ran while one was open for 4% -> 5% of each run, Pallas kernels for 19% -> 26%
where the time goes in v1:
time: 168 us
  Pallas kernels  67 us (40%)
  waiting for transfers between devices  53.2 us (32%)
  starting transfers between devices  33.7 us (20%)
  local copies, waits for them, and re-layouts  9.1 us (5%)
  other arithmetic  1.8 us (1%)
    ppermute x12, waiting for transfers between devices, clockwise(): return lax.ppermute(block, 'ep', self.up)  37.8 us
    pallas_call x4, Pallas kernels, down_mix(): pl.pallas_call(down_kernel, grid_spec=pltpu.PrefetchScalarGridSpec(num_sc...  25.2 us
    pallas_call x2, Pallas kernels, gate_up(): pl.pallas_call(functools.partial(gate_kernel, count=len(blocks), tokens=t...  24.9 us
    ppermute x12, starting transfers between devices, clockwise(): return lax.ppermute(block, 'ep', self.up)  20.1 us
    ppermute x12, waiting for transfers between devices, counter(): return lax.ppermute(block, 'ep', self.down)  14.8 us
    pallas_call x8, Pallas kernels, hop_add(): pl.pallas_call(functools.partial(hop_kernel, plan=tuple(plan)), grid=(1,)...  12.4 us
    ppermute x12, starting transfers between devices, counter(): return lax.ppermute(block, 'ep', self.down)  6.23 us
    unnamed x21, local copies, waits for them, and re-layouts  5.02 us
  transfers between devices with their start and end apart: 36, of which 13 were waited for; matrix products, arithmetic and copies ran while one was open for 5% of the time, Pallas kernels for 26%

profile of v1, /device:TPU:0, one launch (start us, length us, event | category | flops | bytes accessed | tf_op | source)
XLA Modules:
  0.0 167.6 jit_solution(15663459626567248718)
XLA Ops:
  1.3 2.4 %prep.1.refs_0_ = bf16[64,4224]{1,0:T(8,128)(2,1)} custom-call(s32[1]{0:T(128)} %copy.31.lengths, bf16[128,4096]{1,0:T(8,128)(2,1)} %resid.1, bf16[32,128]{1,0:T(8,128)(2,1)} %bitcast.20, f32[8,128]{1,0:T(8,128)} %bitcast.21, s32[8,128]{1,0:T(8,128)} %bitcast.22), custom_call_target="tpu_custom_call" | custom-call | tf_op jit(solution)/shard_map/prep/pallas_call | solution.py:91
  3.7 3.1 %collective-permute-start = (bf16[64,4224]{1,0:T(8,128)(2,1)}, bf16[64,4224]{1,0:T(8,128)(2,1)S(1)}, u32[]{:S(2)}, u32[]{:S(2)}) collective-permute-start(bf16[64,4224]{1,0:T(8,128)(2,1)} %prep.1.refs_0_), channel_id=1, source_target_pairs={{0,4},{4,8},{8,12},{12,14},{14,10},{10,6},{6,2},{2,0},{1,5},{5,9},... | collective-permute-start | bytes 1622024 | tf_op jit(solution)/shard_map/ppermute | solution.py:55
  6.7 12.4 %collective-permute-done.refs_1_ = bf16[64,4224]{1,0:T(8,128)(2,1)S(1)} collective-permute-done((bf16[64,4224]{1,0:T(8,128)(2,1)}, bf16[64,4224]{1,0:T(8,128)(2,1)S(1)}, u32[]{:S(2)}, u32[]{:S(2)}) %collective-permute-start) | collective-permute-done | bytes 540704 | tf_op jit(solution)/shard_map/ppermute | solution.py:55
  19.1 1.8 %collective-permute-start.2 = (bf16[64,4224]{1,0:T(8,128)(2,1)S(1)}, bf16[64,4224]{1,0:T(8,128)(2,1)S(1)}, u32[]{:S(2)}, u32[]{:S(2)}) collective-permute-start(bf16[64,4224]{1,0:T(8,128)(2,1)S(1)} %collective-permute-done.refs_1_), channel_id=1, source_target_pairs={{0,4},{4,8},{8,12},{12,14},{14,10},{10,6},{6,2},{2,0},{1,5},{5,9},... | collective-permute-start | bytes 1622024 | tf_op jit(solution)/shard_map/ppermute | solution.py:55
  21.2 11.4 %collective-permute-done.2.refs_3_ = bf16[64,4224]{1,0:T(8,128)(2,1)S(1)} collective-permute-done((bf16[64,4224]{1,0:T(8,128)(2,1)S(1)}, bf16[64,4224]{1,0:T(8,128)(2,1)S(1)}, u32[]{:S(2)}, u32[]{:S(2)}) %collective-permute-start.2) | collective-permute-done | bytes 540704 | tf_op jit(solution)/shard_map/ppermute | solution.py:55
  36.1 9.1 %collective-permute-done.9.refs_1_ = bf16[64,4224]{1,0:T(8,128)(2,1)S(1)} collective-permute-done((bf16[64,4224]{1,0:T(8,128)(2,1)S(1)}, bf16[64,4224]{1,0:T(8,128)(2,1)S(1)}, u32[]{:S(2)}, u32[]{:S(2)}) %collective-permute-start.9) | collective-permute-done | bytes 540704 | tf_op jit(solution)/shard_map/ppermute | solution.py:55
  46.9 10.0 %collective-permute-done.10.refs_2_ = bf16[64,4224]{1,0:T(8,128)(2,1)S(1)} collective-permute-done((bf16[64,4224]{1,0:T(8,128)(2,1)S(1)}, bf16[64,4224]{1,0:T(8,128)(2,1)S(1)}, u32[]{:S(2)}, u32[]{:S(2)}) %collective-permute-start.10) | collective-permute-done | bytes 540704 | tf_op jit(solution)/shard_map/ppermute | solution.py:58
  60.6 12.3 %gate_up.2 = (bf16[4,160,384]{2,1,0:T(8,128)(2,1)S(1)}, bf16[512,640]{1,0:T(8,128)(2,1)S(1)}) custom-call(s32[1]{0:T(128)} %bitcast.1.peer, bf16[64,4224]{1,0:T(8,128)(2,1)S(1)} %copy-done.3, bf16[64,4224]{1,0:T(8,128)(2,1)S(1)} %collective-permute-done.refs_1_, bf16[64,4224]{1,0:T(8,128)(2,1)S(1)} %collective-permute-done.1.refs_2_, ...), custom_call_target="tpu_custom_call" | custom-call | flops 8000000000 | bytes 25165824 | tf_op jit(solution)/shard_map/gate_up/pallas_call | solution.py:187
  72.9 6.8 %down_mix.4.rest_0_ = bf16[512,2048]{1,0:T(8,128)(2,1)} custom-call(s32[1]{0:T(128)S(6)} %sub.12.half, bf16[4,160,384]{2,1,0:T(8,128)(2,1)S(1)} %get-tuple-element.22.active.refs_12_, bf16[512,640]{1,0:T(8,128)(2,1)S(1)} %get-tuple-element.23.spread, bf16[4,384,4096]{2,1,0:T(8,128)(2,1)} %w_down.7), custom_call_target="tpu_custom_call" | custom-call | flops 3000000000 | bytes 6291456 | tf_op jit(solution)/shard_map/down_mix/pallas_call | solution.py:234
  80.3 5.8 %down_mix.5.rest_0_.refs_5_.refs_6_.refs_0_.refs_1_.kept_0.kept_1 = bf16[512,2048]{1,0:T(8,128)(2,1)S(1)} custom-call(s32[1]{0:T(128)} %bitcast.half, bf16[4,160,384]{2,1,0:T(8,128)(2,1)S(1)} %get-tuple-element.22.active.refs_12_, bf16[512,640]{1,0:T(8,128)(2,1)S(1)} %get-tuple-element.23.spread, bf16[4,384,4096]{2,1,0:T(8,128)(2,1)} %w_down.7, ...), custom_call_target="tpu_custom_call" | custom-call | flops 3000000000 | bytes 6291456 | tf_op jit(solution)/shard_map/down_mix/pallas_call | solution.py:234
  86.1 12.6 %gate_up.3 = (bf16[4,160,384]{2,1,0:T(8,128)(2,1)S(1)}, bf16[512,640]{1,0:T(8,128)(2,1)S(1)}) custom-call(s32[1]{0:T(128)} %bitcast.1.peer, bf16[64,4224]{1,0:T(8,128)(2,1)S(1)} %collective-permute-done.8.refs_0_, bf16[64,4224]{1,0:T(8,128)(2,1)S(1)} %collective-permute-done.9.refs_1_, bf16[64,4224]{1,0:T(8,128)(2,1)S(1)} %collective-permute-done.10.refs_2_, ...), custom_call_target="tpu_custom_call" | custom-call | flops 8000000000 | bytes 25165824 | tf_op jit(solution)/shard_map/gate_up/pallas_call | solution.py:187
  98.8 6.8 %down_mix.6.rest_0_ = bf16[512,2048]{1,0:T(8,128)(2,1)} custom-call(s32[1]{0:T(128)S(6)} %sub.12.half, bf16[4,160,384]{2,1,0:T(8,128)(2,1)S(1)} %get-tuple-element.24.active, bf16[512,640]{1,0:T(8,128)(2,1)S(1)} %get-tuple-element.25.spread, bf16[4,384,4096]{2,1,0:T(8,128)(2,1)} %w_down.7, ...), custom_call_target="tpu_custom_call" | custom-call | flops 3000000000 | bytes 6291456 | tf_op jit(solution)/shard_map/down_mix/pallas_call | solution.py:234
  107.4 5.8 %down_mix.7.refs_0_.refs_2_.refs_1_.refs_5_.refs_6_ = bf16[512,2048]{1,0:T(8,128)(2,1)S(1)} custom-call(s32[1]{0:T(128)} %bitcast.half, bf16[4,160,384]{2,1,0:T(8,128)(2,1)S(1)} %get-tuple-element.24.active, bf16[512,640]{1,0:T(8,128)(2,1)S(1)} %get-tuple-element.25.spread, bf16[4,384,4096]{2,1,0:T(8,128)(2,1)} %w_down.7, bf16[512,2048]{1,0:T(8,128)(2,1)} %down_mix.6.rest_0_), custom_call_target="tpu_custom_call" | custom-call | flops 3000000000 | bytes 6291456 | tf_op jit(solution)/shard_map/down_mix/pallas_call | solution.py:234
  120.7 1.9 %hop_add.9 = (bf16[128,1024]{1,0:T(8,128)(2,1)}, bf16[128,1024]{1,0:T(8,128)(2,1)S(1)}) custom-call(bf16[512,2048]{1,0:T(8,128)(2,1)S(1)} %down_mix.7.refs_0_.refs_2_.refs_1_.refs_5_.refs_6_, bf16[512,2048]{1,0:T(8,128)(2,1)S(1)} %down_mix.7.refs_0_.refs_2_.refs_1_.refs_5_.refs_6_, ...), custom_call_target="tpu_custom_call" | custom-call | flops 1000000000 | bytes 2621440 | tf_op jit(solution)/shard_map/hop_add/pallas_call | solution.py:305
  124.6 2.0 %hop_add.13 = (bf16[128,1024]{1,0:T(8,128)(2,1)}, bf16[128,1024]{1,0:T(8,128)(2,1)}) custom-call(bf16[512,2048]{1,0:T(8,128)(2,1)S(1)} %down_mix.7.refs_0_.refs_2_.refs_1_.refs_5_.refs_6_, bf16[512,2048]{1,0:T(8,128)(2,1)S(1)} %down_mix.7.refs_0_.refs_2_.refs_1_.refs_5_.refs_6_, ...), custom_call_target="tpu_custom_call" | custom-call | flops 1000000000 | bytes 2621440 | tf_op jit(solution)/shard_map/hop_add/pallas_call | solution.py:305
  129.6 1.7 %reshape.171 = bf16[8,2,8320]{2,1,0:T(2,128)(2,1)} reshape(bf16[16,8320]{1,0:T(8,128)(2,1)} %convolution_convert_fusion) | data formatting | bytes 532480 | tf_op jit(solution)/shard_map/reshape | solution.py:408
  131.3 4.8 %all-to-all-start = ((bf16[8,2,8320]{2,1,0:T(2,128)(2,1)}), bf16[8,2,8320]{2,1,0:T(2,128)(2,1)}, u32[]{:S(2)}, u32[]{:S(2)}) async-start(bf16[8,2,8320]{2,1,0:T(2,128)(2,1)} %reshape.171), calls=%async_computation | async-start | bytes 532480 | tf_op jit(solution)/shard_map/all_to_all | solution.py:409
  137.7 1.9 %hop_add.10 = (bf16[128,1024]{1,0:T(8,128)(2,1)}, bf16[128,1024]{1,0:T(8,128)(2,1)S(1)}) custom-call(bf16[512,2048]{1,0:T(8,128)(2,1)S(1)} %down_mix.7.refs_0_.refs_2_.refs_1_.refs_5_.refs_6_, bf16[512,2048]{1,0:T(8,128)(2,1)S(1)} %down_mix.7.refs_0_.refs_2_.refs_1_.refs_5_.refs_6_, ...), custom_call_target="tpu_custom_call" | custom-call | flops 1000000000 | bytes 2621440 | tf_op jit(solution)/shard_map/hop_add/pallas_call | solution.py:305
  139.6 2.0 %collective-permute-start.23 = (bf16[128,1024]{1,0:T(8,128)(2,1)}, bf16[128,1024]{1,0:T(8,128)(2,1)S(1)}, u32[]{:S(2)}, u32[]{:S(2)}) collective-permute-start(bf16[128,1024]{1,0:T(8,128)(2,1)} %get-tuple-element.30), channel_id=1, source_target_pairs={{0,4},{4,8},{8,12},{12,14},{14,10},{10,6},{6,2},{2,0},{1,5},{5,9},... | collective-permute-start | bytes 786440 | tf_op jit(solution)/shard_map/ppermute | solution.py:55
  141.7 2.0 %hop_add.14 = (bf16[128,1024]{1,0:T(8,128)(2,1)}, bf16[128,1024]{1,0:T(8,128)(2,1)}) custom-call(bf16[512,2048]{1,0:T(8,128)(2,1)S(1)} %down_mix.7.refs_0_.refs_2_.refs_1_.refs_5_.refs_6_, bf16[512,2048]{1,0:T(8,128)(2,1)S(1)} %down_mix.7.refs_0_.refs_2_.refs_1_.refs_5_.refs_6_, ...), custom_call_target="tpu_custom_call" | custom-call | flops 1000000000 | bytes 2621440 | tf_op jit(solution)/shard_map/hop_add/pallas_call | solution.py:305
  143.7 2.0 %collective-permute-start.31 = (bf16[128,1024]{1,0:T(8,128)(2,1)}, bf16[128,1024]{1,0:T(8,128)(2,1)S(1)}, u32[]{:S(2)}, u32[]{:S(2)}) collective-permute-start(bf16[128,1024]{1,0:T(8,128)(2,1)} %get-tuple-element.38), channel_id=1, source_target_pairs={{0,4},{4,8},{8,12},{12,14},{14,10},{10,6},{6,2},{2,0},{1,5},{5,9},... | collective-permute-start | bytes 786440 | tf_op jit(solution)/shard_map/ppermute | solution.py:55
  147.2 2.1 %collective-permute-done.23.refs_4_ = bf16[128,1024]{1,0:T(8,128)(2,1)S(1)} collective-permute-done((bf16[128,1024]{1,0:T(8,128)(2,1)}, bf16[128,1024]{1,0:T(8,128)(2,1)S(1)}, u32[]{:S(2)}, u32[]{:S(2)}) %collective-permute-start.23) | collective-permute-done | bytes 262176 | tf_op jit(solution)/shard_map/ppermute | solution.py:55
  157.1 2.0 %collective-permute-start.33 = (bf16[128,1024]{1,0:T(8,128)(2,1)S(1)}, bf16[128,1024]{1,0:T(8,128)(2,1)S(1)}, u32[]{:S(2)}, u32[]{:S(2)}) collective-permute-start(bf16[128,1024]{1,0:T(8,128)(2,1)S(1)} %get-tuple-element.40), channel_id=1, source_target_pairs={{0,4},{4,8},{8,12},{12,14},{14,10},{10,6},{6,2},{2,0},{1,5},{5,9},... | collective-permute-start | bytes 786440 | tf_op jit(solution)/shard_map/ppermute | solution.py:55
  165.5 2.1 %last_add.1 = bf16[128,2048]{1,0:T(8,128)(2,1)} custom-call(bf16[512,2048]{1,0:T(8,128)(2,1)S(1)} %copy-done.2, bf16[512,2048]{1,0:T(8,128)(2,1)S(1)} %copy-done.2, bf16[512,2048]{1,0:T(8,128)(2,1)} %collective-permute-done.7.refs_7_.refs_8_.refs_2_.refs_3_.taken_0.taken_1, ...), custom_call_target="tpu_custom_call" | custom-call | tf_op jit(solution)/shard_map/last_add/pallas_call | solution.py:337
  (113 shorter events, 41.1 us)
Async XLA Ops:
  3.7 15.5 %collective-permute-start = (bf16[64,4224]{1,0:T(8,128)(2,1)}, bf16[64,4224]{1,0:T(8,128)(2,1)S(1)}, u32[]{:S(2)}, u32[]{:S(2)}) collective-permute-start(bf16[64,4224]{1,0:T(8,128)(2,1)} %prep.1.refs_0_), channel_id=1, source_target_pairs={{0,4},{4,8},{8,12},{12,14},{14,10},{10,6},{6,2},{2,0},{1,5},{5,9},... | collective-permute-start | bytes 1622024 | tf_op jit(solution)/shard_map/ppermute | solution.py:55
  6.7 14.2 %collective-permute-start.1 = (bf16[64,4224]{1,0:T(8,128)(2,1)}, bf16[64,4224]{1,0:T(8,128)(2,1)S(1)}, u32[]{:S(2)}, u32[]{:S(2)}) collective-permute-start(bf16[64,4224]{1,0:T(8,128)(2,1)} %prep.1.refs_0_), channel_id=1, source_target_pairs={{4,0},{8,4},{12,8},{14,12},{10,14},{6,10},{2,6},{0,2},{5,1},{9,5},... | collective-permute-start | bytes 1622024 | tf_op jit(solution)/shard_map/ppermute | solution.py:58
  19.1 13.4 %collective-permute-start.2 = (bf16[64,4224]{1,0:T(8,128)(2,1)S(1)}, bf16[64,4224]{1,0:T(8,128)(2,1)S(1)}, u32[]{:S(2)}, u32[]{:S(2)}) collective-permute-start(bf16[64,4224]{1,0:T(8,128)(2,1)S(1)} %collective-permute-done.refs_1_), channel_id=1, source_target_pairs={{0,4},{4,8},{8,12},{12,14},{14,10},{10,6},{6,2},{2,0},{1,5},{5,9},... | collective-permute-start | bytes 1622024 | tf_op jit(solution)/shard_map/ppermute | solution.py:55
  20.9 14.7 %collective-permute-start.8 = (bf16[64,4224]{1,0:T(8,128)(2,1)S(1)}, bf16[64,4224]{1,0:T(8,128)(2,1)S(1)}, u32[]{:S(2)}, u32[]{:S(2)}) collective-permute-start(bf16[64,4224]{1,0:T(8,128)(2,1)S(1)} %collective-permute-done.1.refs_2_), channel_id=1, source_target_pairs={{4,0},{8,4},{12,8},{14,12},{10,14},{6,10},{2,6},{0,2},{5,1},{9,5},... | collective-permute-start | bytes 1622024 | tf_op jit(solution)/shard_map/ppermute | solution.py:58
  32.6 12.6 %collective-permute-start.9 = (bf16[64,4224]{1,0:T(8,128)(2,1)S(1)}, bf16[64,4224]{1,0:T(8,128)(2,1)S(1)}, u32[]{:S(2)}, u32[]{:S(2)}) collective-permute-start(bf16[64,4224]{1,0:T(8,128)(2,1)S(1)} %collective-permute-done.2.refs_3_), channel_id=1, source_target_pairs={{0,4},{4,8},{8,12},{12,14},{14,10},{10,6},{6,2},{2,0},{1,5},{5,9},... | collective-permute-start | bytes 1622024 | tf_op jit(solution)/shard_map/ppermute | solution.py:55
  34.1 22.8 %collective-permute-start.3 = (bf16[64,4224]{1,0:T(8,128)(2,1)}, bf16[64,4224]{1,0:T(8,128)(2,1)}, u32[]{:S(2)}, u32[]{:S(2)}) collective-permute-start(bf16[64,4224]{1,0:T(8,128)(2,1)} %prep.1.refs_0_), channel_id=1, source_target_pairs={{0,1},{1,0},{2,3},{3,2},{4,5},{5,4},{6,7},{7,6},{8,9},{9,8},{10,11... | collective-permute-start | bytes 1622024 | tf_op jit(solution)/shard_map/ppermute | solution.py:62
  35.0 22.9 %collective-permute-start.4 = (bf16[64,4224]{1,0:T(8,128)(2,1)S(1)}, bf16[64,4224]{1,0:T(8,128)(2,1)S(1)}, u32[]{:S(2)}, u32[]{:S(2)}) collective-permute-start(bf16[64,4224]{1,0:T(8,128)(2,1)S(1)} %collective-permute-done.refs_1_), channel_id=1, source_target_pairs={{0,1},{1,0},{2,3},{3,2},{4,5},{5,4},{6,7},{7,6},{8,9},{9,8},{10,11... | collective-permute-start | bytes 1622024 | tf_op jit(solution)/shard_map/ppermute | solution.py:62
  35.6 23.4 %collective-permute-start.5 = (bf16[64,4224]{1,0:T(8,128)(2,1)S(1)}, bf16[64,4224]{1,0:T(8,128)(2,1)S(1)}, u32[]{:S(2)}, u32[]{:S(2)}) collective-permute-start(bf16[64,4224]{1,0:T(8,128)(2,1)S(1)} %collective-permute-done.1.refs_2_), channel_id=1, source_target_pairs={{0,1},{1,0},{2,3},{3,2},{4,5},{5,4},{6,7},{7,6},{8,9},{9,8},{10,11... | collective-permute-start | bytes 1622024 | tf_op jit(solution)/shard_map/ppermute | solution.py:62
  35.7 23.3 %collective-permute-start.6 = (bf16[64,4224]{1,0:T(8,128)(2,1)S(1)}, bf16[64,4224]{1,0:T(8,128)(2,1)S(1)}, u32[]{:S(2)}, u32[]{:S(2)}) collective-permute-start(bf16[64,4224]{1,0:T(8,128)(2,1)S(1)} %collective-permute-done.2.refs_3_), channel_id=1, source_target_pairs={{0,1},{1,0},{2,3},{3,2},{4,5},{5,4},{6,7},{7,6},{8,9},{9,8},{10,11... | collective-permute-start | bytes 1622024 | tf_op jit(solution)/shard_map/ppermute | solution.py:62
  45.2 11.7 %collective-permute-start.10 = (bf16[64,4224]{1,0:T(8,128)(2,1)S(1)}, bf16[64,4224]{1,0:T(8,128)(2,1)S(1)}, u32[]{:S(2)}, u32[]{:S(2)}) collective-permute-start(bf16[64,4224]{1,0:T(8,128)(2,1)S(1)} %collective-permute-done.8.refs_0_), channel_id=1, source_target_pairs={{4,0},{8,4},{12,8},{14,12},{10,14},{6,10},{2,6},{0,2},{5,1},{9,5},... | collective-permute-start | bytes 1622024 | tf_op jit(solution)/shard_map/ppermute | solution.py:58
  56.9 29.2 %collective-permute-start.13 = (bf16[64,4224]{1,0:T(8,128)(2,1)S(1)}, bf16[64,4224]{1,0:T(8,128)(2,1)S(1)}, u32[]{:S(2)}, u32[]{:S(2)}) collective-permute-start(bf16[64,4224]{1,0:T(8,128)(2,1)S(1)} %collective-permute-done.8.refs_0_), channel_id=1, source_target_pairs={{0,1},{1,0},{2,3},{3,2},{4,5},{5,4},{6,7},{7,6},{8,9},{9,8},{10,11... | collective-permute-start | bytes 1622024 | tf_op jit(solution)/shard_map/ppermute | solution.py:62
  56.9 22.8 %collective-permute-start.11 = (bf16[32,4224]{1,0:T(8,128)(2,1)S(1)}, bf16[32,4224]{1,0:T(8,128)(2,1)S(1)}, u32[]{:S(2)}, u32[]{:S(2)}) collective-permute-start(bf16[32,4224]{1,0:T(8,128)(2,1)S(1)} %slice.24), channel_id=1, source_target_pairs={{0,4},{4,8},{8,12},{12,14},{14,10},{10,6},{6,2},{2,0},{1,5},{5,9},... | collective-permute-start | bytes 811016 | tf_op jit(solution)/shard_map/ppermute | solution.py:55
  57.9 21.9 %collective-permute-start.12 = (bf16[32,4224]{1,0:T(8,128)(2,1)S(1)}, bf16[32,4224]{1,0:T(8,128)(2,1)S(1)}, u32[]{:S(2)}, u32[]{:S(2)}) collective-permute-start(bf16[32,4224]{1,0:T(8,128)(2,1)S(1)} %slice.25), channel_id=1, source_target_pairs={{4,0},{8,4},{12,8},{14,12},{10,14},{6,10},{2,6},{0,2},{5,1},{9,5},... | collective-permute-start | bytes 811016 | tf_op jit(solution)/shard_map/ppermute | solution.py:58
  59.0 27.0 %collective-permute-start.14 = (bf16[64,4224]{1,0:T(8,128)(2,1)S(1)}, bf16[64,4224]{1,0:T(8,128)(2,1)S(1)}, u32[]{:S(2)}, u32[]{:S(2)}) collective-permute-start(bf16[64,4224]{1,0:T(8,128)(2,1)S(1)} %collective-permute-done.9.refs_1_), channel_id=1, source_target_pairs={{0,1},{1,0},{2,3},{3,2},{4,5},{5,4},{6,7},{7,6},{8,9},{9,8},{10,11... | collective-permute-start | bytes 1622024 | tf_op jit(solution)/shard_map/ppermute | solution.py:62
  59.0 27.0 %collective-permute-start.15 = (bf16[64,4224]{1,0:T(8,128)(2,1)S(1)}, bf16[64,4224]{1,0:T(8,128)(2,1)S(1)}, u32[]{:S(2)}, u32[]{:S(2)}) collective-permute-start(bf16[64,4224]{1,0:T(8,128)(2,1)S(1)} %collective-permute-done.10.refs_2_), channel_id=1, source_target_pairs={{0,1},{1,0},{2,3},{3,2},{4,5},{5,4},{6,7},{7,6},{8,9},{9,8},{10,11... | collective-permute-start | bytes 1622024 | tf_op jit(solution)/shard_map/ppermute | solution.py:62
  106.6 29.5 %collective-permute-start.7 = (bf16[512,2048]{1,0:T(8,128)(2,1)}, bf16[512,2048]{1,0:T(8,128)(2,1)}, u32[]{:S(2)}, u32[]{:S(2)}) collective-permute-start(bf16[512,2048]{1,0:T(8,128)(2,1)} %down_mix.4.rest_0_), channel_id=1, source_target_pairs={{0,1},{1,0},{2,3},{3,2},{4,5},{5,4},{6,7},{7,6},{8,9},{9,8},{10,11... | collective-permute-start | bytes 6291464 | tf_op jit(solution)/shard_map/ppermute | solution.py:62
  122.6 13.6 %collective-permute-start.21 = (bf16[128,1024]{1,0:T(8,128)(2,1)}, bf16[128,1024]{1,0:T(8,128)(2,1)S(1)}, u32[]{:S(2)}, u32[]{:S(2)}) collective-permute-start(bf16[128,1024]{1,0:T(8,128)(2,1)} %get-tuple-element.28), channel_id=1, source_target_pairs={{0,4},{4,8},{8,12},{12,14},{14,10},{10,6},{6,2},{2,0},{1,5},{5,9},... | collective-permute-start | bytes 786440 | tf_op jit(solution)/shard_map/ppermute | solution.py:55
  124.1 12.0 %collective-permute-start.22 = (bf16[128,1024]{1,0:T(8,128)(2,1)S(1)}, bf16[128,1024]{1,0:T(8,128)(2,1)S(1)}, u32[]{:S(2)}, u32[]{:S(2)}) collective-permute-start(bf16[128,1024]{1,0:T(8,128)(2,1)S(1)} %get-tuple-element.29), channel_id=1, source_target_pairs={{4,0},{8,4},{12,8},{14,12},{10,14},{6,10},{2,6},{0,2},{5,1},{9,5},... | collective-permute-start | bytes 786440 | tf_op jit(solution)/shard_map/ppermute | solution.py:58
  126.6 15.1 %collective-permute-start.29 = (bf16[128,1024]{1,0:T(8,128)(2,1)}, bf16[128,1024]{1,0:T(8,128)(2,1)S(1)}, u32[]{:S(2)}, u32[]{:S(2)}) collective-permute-start(bf16[128,1024]{1,0:T(8,128)(2,1)} %get-tuple-element.36), channel_id=1, source_target_pairs={{0,4},{4,8},{8,12},{12,14},{14,10},{10,6},{6,2},{2,0},{1,5},{5,9},... | collective-permute-start | bytes 786440 | tf_op jit(solution)/shard_map/ppermute | solution.py:55
  128.1 13.6 %collective-permute-start.30 = (bf16[128,1024]{1,0:T(8,128)(2,1)}, bf16[128,1024]{1,0:T(8,128)(2,1)S(1)}, u32[]{:S(2)}, u32[]{:S(2)}) collective-permute-start(bf16[128,1024]{1,0:T(8,128)(2,1)} %get-tuple-element.37), channel_id=1, source_target_pairs={{4,0},{8,4},{12,8},{14,12},{10,14},{6,10},{2,6},{0,2},{5,1},{9,5},... | collective-permute-start | bytes 786440 | tf_op jit(solution)/shard_map/ppermute | solution.py:58
  131.3 14.8 %all-to-all-start = ((bf16[8,2,8320]{2,1,0:T(2,128)(2,1)}), bf16[8,2,8320]{2,1,0:T(2,128)(2,1)}, u32[]{:S(2)}, u32[]{:S(2)}) async-start(bf16[8,2,8320]{2,1,0:T(2,128)(2,1)} %reshape.171), calls=%async_computation | async-start | bytes 532480 | tf_op jit(solution)/shard_map/all_to_all | solution.py:409
  139.6 9.7 %collective-permute-start.23 = (bf16[128,1024]{1,0:T(8,128)(2,1)}, bf16[128,1024]{1,0:T(8,128)(2,1)S(1)}, u32[]{:S(2)}, u32[]{:S(2)}) collective-permute-start(bf16[128,1024]{1,0:T(8,128)(2,1)} %get-tuple-element.30), channel_id=1, source_target_pairs={{0,4},{4,8},{8,12},{12,14},{14,10},{10,6},{6,2},{2,0},{1,5},{5,9},... | collective-permute-start | bytes 786440 | tf_op jit(solution)/shard_map/ppermute | solution.py:55
  143.7 12.1 %collective-permute-start.31 = (bf16[128,1024]{1,0:T(8,128)(2,1)}, bf16[128,1024]{1,0:T(8,128)(2,1)S(1)}, u32[]{:S(2)}, u32[]{:S(2)}) collective-permute-start(bf16[128,1024]{1,0:T(8,128)(2,1)} %get-tuple-element.38), channel_id=1, source_target_pairs={{0,4},{4,8},{8,12},{12,14},{14,10},{10,6},{6,2},{2,0},{1,5},{5,9},... | collective-permute-start | bytes 786440 | tf_op jit(solution)/shard_map/ppermute | solution.py:55
  145.7 10.1 %collective-permute-start.32 = (bf16[128,1024]{1,0:T(8,128)(2,1)}, bf16[128,1024]{1,0:T(8,128)(2,1)S(1)}, u32[]{:S(2)}, u32[]{:S(2)}) collective-permute-start(bf16[128,1024]{1,0:T(8,128)(2,1)} %get-tuple-element.39), channel_id=1, source_target_pairs={{4,0},{8,4},{12,8},{14,12},{10,14},{6,10},{2,6},{0,2},{5,1},{9,5},... | collective-permute-start | bytes 786440 | tf_op jit(solution)/shard_map/ppermute | solution.py:58
  (22 other events, 160.3 us)

commit v2 on v1

--- a/solution.py
+++ b/solution.py
@@ -226,7 +226,7 @@
     out[...] = jnp.dot(spread[...], held[...], preferred_element_type=jnp.float32).astype(out.dtype)
 
 
-def down_mix(half, active, spread, w_down, columns, dtype, after=(), step=512):
+def down_mix(half, active, spread, w_down, columns, dtype, after=(), step=1024):
     local, capacity, units = active.shape
     tokens = spread.shape[0]
     steps = columns // step
@@ -453,16 +453,18 @@
         blocks = [piece for pieces in found[span] + swapped[span] for piece in pieces]
         after = groups[-1][:1] if groups else ()
         groups.append(gate_up(peer, blocks, w_gate, w_up, levels, after))
-    sums = [None, None]
-    after = ()
-    for group in (0, 1):
+
+    def half_sums(side, group, after):
         active, spread = groups[group]
-        given = down_mix(1 - mine, active, spread, w_down, col_width, jnp.bfloat16, after)
-        taken = swap_section(given)
-        kept = down_mix(mine, active, spread, w_down, col_width, jnp.bfloat16, (given,))
-        sums[group] = (kept, taken)
-        after = (kept,)
-
+        return down_mix(side, active, spread, w_down, col_width, jnp.bfloat16, after)
+
+    given_near = half_sums(1 - mine, 0, ())
+    given_far = half_sums(1 - mine, 1, (given_near,))
+    kept_far = half_sums(mine, 1, (given_far,))
+    kept_near = half_sums(mine, 0, (kept_far,))
+    taken_near = swap_section(given_near)
+    taken_far = swap_section(given_far)
+    sums = [(kept_near, taken_near), (kept_far, taken_far)]
     return (scatter_ring(ring, sums, rows, PARTS), kv_cache)
 
 

time: 168 us -> 172 us (1.024)
  local copies, waits for them, and re-layouts: 9.1 us -> 13.2 us
  starting transfers between devices: 33.7 us -> 35.9 us
  waiting for transfers between devices: 53.2 us -> 51.1 us
    ppermute x12, waiting for transfers between devices: 37.8 us -> 34 us  [clockwise(): return lax.ppermute(block, 'ep', self.up)]
    unnamed x21 -> x29, local copies, waits for them, and re-layouts: 5.02 us -> 8.43 us
    ppermute x12, starting transfers between devices: 20.1 us -> 23.1 us  [clockwise(): return lax.ppermute(block, 'ep', self.up)]
    ppermute x12, waiting for transfers between devices: 14.8 us -> 17.1 us  [counter(): return lax.ppermute(block, 'ep', self.down)]
  transfers between devices with their start and end apart: 36 -> 36, of which waited for: 13 -> 12; matrix products, arithmetic and copies ran while one was open for 5% -> 6% of each run, Pallas kernels for 26% -> 24%
where the time goes in v2:
time: 172 us
  Pallas kernels  65.5 us (38%)
  waiting for transfers between devices  51.1 us (30%)
  starting transfers between devices  35.9 us (21%)
  local copies, waits for them, and re-layouts  13.2 us (8%)
  other arithmetic  3.28 us (2%)
    ppermute x12, waiting for transfers between devices, clockwise(): return lax.ppermute(block, 'ep', self.up)  34 us
    pallas_call x2, Pallas kernels, gate_up(): pl.pallas_call(functools.partial(gate_kernel, count=len(blocks), tokens=t...  24.8 us
    pallas_call x4, Pallas kernels, down_mix(): pl.pallas_call(down_kernel, grid_spec=pltpu.PrefetchScalarGridSpec(num_sc...  23.7 us
    ppermute x12, starting transfers between devices, clockwise(): return lax.ppermute(block, 'ep', self.up)  23.1 us
    ppermute x12, waiting for transfers between devices, counter(): return lax.ppermute(block, 'ep', self.down)  17.1 us
    pallas_call x8, Pallas kernels, hop_add(): pl.pallas_call(functools.partial(hop_kernel, plan=tuple(plan)), grid=(1,)...  12.6 us
    unnamed x29, local copies, waits for them, and re-layouts  8.43 us
    all_to_all x1, starting transfers between devices, kv_part(): got = lax.all_to_all(sent, 'ep', split_axis=0, concat_axis=0, tiled=True)  5.23 us
  transfers between devices with their start and end apart: 36, of which 12 were waited for; matrix products, arithmetic and copies ran while one was open for 6% of the time, Pallas kernels for 24%

profile of v2, /device:TPU:0, one launch (start us, length us, event | category | flops | bytes accessed | tf_op | source)
XLA Modules:
  0.0 171.6 jit_solution(8663288685856216565)
XLA Ops:
  1.3 2.4 %prep.1.refs_0_ = bf16[64,4224]{1,0:T(8,128)(2,1)} custom-call(s32[1]{0:T(128)} %copy.31.lengths, bf16[128,4096]{1,0:T(8,128)(2,1)} %resid.1, bf16[32,128]{1,0:T(8,128)(2,1)} %bitcast.20, f32[8,128]{1,0:T(8,128)} %bitcast.21, s32[8,128]{1,0:T(8,128)} %bitcast.22), custom_call_target="tpu_custom_call" | custom-call | tf_op jit(solution)/shard_map/prep/pallas_call | solution.py:91
  3.7 3.1 %collective-permute-start = (bf16[64,4224]{1,0:T(8,128)(2,1)}, bf16[64,4224]{1,0:T(8,128)(2,1)S(1)}, u32[]{:S(2)}, u32[]{:S(2)}) collective-permute-start(bf16[64,4224]{1,0:T(8,128)(2,1)} %prep.1.refs_0_), channel_id=1, source_target_pairs={{0,4},{4,8},{8,12},{12,14},{14,10},{10,6},{6,2},{2,0},{1,5},{5,9},... | collective-permute-start | bytes 1622024 | tf_op jit(solution)/shard_map/ppermute | solution.py:55
  6.7 12.4 %collective-permute-done.refs_1_ = bf16[64,4224]{1,0:T(8,128)(2,1)S(1)} collective-permute-done((bf16[64,4224]{1,0:T(8,128)(2,1)}, bf16[64,4224]{1,0:T(8,128)(2,1)S(1)}, u32[]{:S(2)}, u32[]{:S(2)}) %collective-permute-start) | collective-permute-done | bytes 540704 | tf_op jit(solution)/shard_map/ppermute | solution.py:55
  21.2 11.4 %collective-permute-done.2.refs_3_ = bf16[64,4224]{1,0:T(8,128)(2,1)S(1)} collective-permute-done((bf16[64,4224]{1,0:T(8,128)(2,1)S(1)}, bf16[64,4224]{1,0:T(8,128)(2,1)S(1)}, u32[]{:S(2)}, u32[]{:S(2)}) %collective-permute-start.2) | collective-permute-done | bytes 540704 | tf_op jit(solution)/shard_map/ppermute | solution.py:55
  37.0 8.2 %collective-permute-done.8.refs_1_ = bf16[64,4224]{1,0:T(8,128)(2,1)S(1)} collective-permute-done((bf16[64,4224]{1,0:T(8,128)(2,1)S(1)}, bf16[64,4224]{1,0:T(8,128)(2,1)S(1)}, u32[]{:S(2)}, u32[]{:S(2)}) %collective-permute-start.8) | collective-permute-done | bytes 540704 | tf_op jit(solution)/shard_map/ppermute | solution.py:55
  47.3 9.6 %collective-permute-done.9.refs_2_ = bf16[64,4224]{1,0:T(8,128)(2,1)S(1)} collective-permute-done((bf16[64,4224]{1,0:T(8,128)(2,1)S(1)}, bf16[64,4224]{1,0:T(8,128)(2,1)S(1)}, u32[]{:S(2)}, u32[]{:S(2)}) %collective-permute-start.9) | collective-permute-done | bytes 540704 | tf_op jit(solution)/shard_map/ppermute | solution.py:58
  63.4 12.4 %gate_up.2 = (bf16[4,160,384]{2,1,0:T(8,128)(2,1)S(1)}, bf16[512,640]{1,0:T(8,128)(2,1)S(1)}) custom-call(s32[1]{0:T(128)} %bitcast.1.peer, bf16[64,4224]{1,0:T(8,128)(2,1)S(1)} %copy-done.6, bf16[64,4224]{1,0:T(8,128)(2,1)S(1)} %collective-permute-done.refs_1_, bf16[64,4224]{1,0:T(8,128)(2,1)S(1)} %collective-permute-done.1.refs_2_, ...), custom_call_target="tpu_custom_call" | custom-call | flops 8000000000 | bytes 25165824 | tf_op jit(solution)/shard_map/gate_up/pallas_call | solution.py:187
  76.4 6.3 %down_mix.4.rest_0_ = bf16[512,2048]{1,0:T(8,128)(2,1)} custom-call(s32[1]{0:T(128)S(6)} %sub.12.half, bf16[4,160,384]{2,1,0:T(8,128)(2,1)S(1)} %get-tuple-element.22.refs_12_.active, bf16[512,640]{1,0:T(8,128)(2,1)S(1)} %get-tuple-element.23.spread, bf16[4,384,4096]{2,1,0:T(8,128)(2,1)} %w_down.7), custom_call_target="tpu_custom_call" | custom-call | flops 3000000000 | bytes 6291456 | tf_op jit(solution)/shard_map/down_mix/pallas_call | solution.py:234
  82.7 12.4 %gate_up.3 = (bf16[4,160,384]{2,1,0:T(8,128)(2,1)S(1)}, bf16[512,640]{1,0:T(8,128)(2,1)S(1)}) custom-call(s32[1]{0:T(128)} %bitcast.1.peer, bf16[64,4224]{1,0:T(8,128)(2,1)S(1)} %collective-permute-done.7.refs_0_, bf16[64,4224]{1,0:T(8,128)(2,1)S(1)} %collective-permute-done.8.refs_1_, bf16[64,4224]{1,0:T(8,128)(2,1)S(1)} %collective-permute-done.9.refs_2_, ...), custom_call_target="tpu_custom_call" | custom-call | flops 8000000000 | bytes 25165824 | tf_op jit(solution)/shard_map/gate_up/pallas_call | solution.py:187
  95.1 6.7 %down_mix.5.rest_0_ = bf16[512,2048]{1,0:T(8,128)(2,1)} custom-call(s32[1]{0:T(128)S(6)} %sub.12.half, bf16[4,160,384]{2,1,0:T(8,128)(2,1)S(1)} %get-tuple-element.24.active, bf16[512,640]{1,0:T(8,128)(2,1)S(1)} %get-tuple-element.25.spread, bf16[4,384,4096]{2,1,0:T(8,128)(2,1)} %w_down.7, bf16[512,2048]{1,0:T(8,128)(2,1)} %down_mix.4.rest_0_), custom_call_target="tpu_custom_call" | custom-call | flops 3000000000 | bytes 6291456 | tf_op jit(solution)/shard_map/down_mix/pallas_call | solution.py:234
  106.9 5.4 %down_mix.6.rest_0_.refs_0_.refs_2_.refs_1_.refs_5_.refs_6_ = bf16[512,2048]{1,0:T(8,128)(2,1)S(1)} custom-call(s32[1]{0:T(128)} %bitcast.half, bf16[4,160,384]{2,1,0:T(8,128)(2,1)S(1)} %copy-done.5, bf16[512,640]{1,0:T(8,128)(2,1)S(1)} %copy-done.3, bf16[4,384,4096]{2,1,0:T(8,128)(2,1)} %w_down.7, bf16[512,2048]{1,0:T(8,128)(2,1)} %down_mix.5.rest_0_), custom_call_target="tpu_custom_call" | custom-call | flops 3000000000 | bytes 6291456 | tf_op jit(solution)/shard_map/down_mix/pallas_call | solution.py:234
  122.5 5.2 %all-to-all-start = ((bf16[8,2,8320]{2,1,0:T(2,128)(2,1)}), bf16[8,2,8320]{2,1,0:T(2,128)(2,1)}, u32[]{:S(2)}, u32[]{:S(2)}) async-start(bf16[8,2,8320]{2,1,0:T(2,128)(2,1)} %reshape.171), calls=%async_computation | async-start | bytes 532480 | tf_op jit(solution)/shard_map/all_to_all | solution.py:409
  129.1 2.1 %collective-permute-start.21 = (bf16[128,1024]{1,0:T(8,128)(2,1)S(1)}, bf16[128,1024]{1,0:T(8,128)(2,1)S(1)}, u32[]{:S(2)}, u32[]{:S(2)}) collective-permute-start(bf16[128,1024]{1,0:T(8,128)(2,1)S(1)} %get-tuple-element.28), channel_id=1, source_target_pairs={{0,4},{4,8},{8,12},{12,14},{14,10},{10,6},{6,2},{2,0},{1,5},{5,9},... | collective-permute-start | bytes 786440 | tf_op jit(solution)/shard_map/ppermute | solution.py:55
  132.5 2.0 %collective-permute-start.29 = (bf16[128,1024]{1,0:T(8,128)(2,1)S(1)}, bf16[128,1024]{1,0:T(8,128)(2,1)S(1)}, u32[]{:S(2)}, u32[]{:S(2)}) collective-permute-start(bf16[128,1024]{1,0:T(8,128)(2,1)S(1)} %get-tuple-element.36), channel_id=1, source_target_pairs={{0,4},{4,8},{8,12},{12,14},{14,10},{10,6},{6,2},{2,0},{1,5},{5,9},... | collective-permute-start | bytes 786440 | tf_op jit(solution)/shard_map/ppermute | solution.py:55
  134.6 5.4 %down_mix.7.refs_5_.refs_6_.refs_0_.refs_1_.kept_0.kept_1 = bf16[512,2048]{1,0:T(8,128)(2,1)S(1)} custom-call(s32[1]{0:T(128)} %bitcast.half, bf16[4,160,384]{2,1,0:T(8,128)(2,1)S(1)} %get-tuple-element.22.refs_12_.active, bf16[512,640]{1,0:T(8,128)(2,1)S(1)} %get-tuple-element.23.spread, bf16[4,384,4096]{2,1,0:T(8,128)(2,1)} %w_down.7, ...), custom_call_target="tpu_custom_call" | custom-call | flops 3000000000 | bytes 6291456 | tf_op jit(solution)/shard_map/down_mix/pallas_call | solution.py:234
  141.4 1.9 %hop_add.10 = (bf16[128,1024]{1,0:T(8,128)(2,1)}, bf16[128,1024]{1,0:T(8,128)(2,1)S(1)}) custom-call(bf16[512,2048]{1,0:T(8,128)(2,1)S(1)} %down_mix.6.rest_0_.refs_0_.refs_2_.refs_1_.refs_5_.refs_6_, bf16[512,2048]{1,0:T(8,128)(2,1)S(1)} %down_mix.6.rest_0_.refs_0_.refs_2_.refs_1_.refs_5_.refs_6_, ...), custom_call_target="tpu_custom_call" | custom-call | flops 1000000000 | bytes 2621440 | tf_op jit(solution)/shard_map/hop_add/pallas_call | solution.py:305
  143.3 2.2 %collective-permute-start.23 = (bf16[128,1024]{1,0:T(8,128)(2,1)}, bf16[128,1024]{1,0:T(8,128)(2,1)S(1)}, u32[]{:S(2)}, u32[]{:S(2)}) collective-permute-start(bf16[128,1024]{1,0:T(8,128)(2,1)} %get-tuple-element.30), channel_id=1, source_target_pairs={{0,4},{4,8},{8,12},{12,14},{14,10},{10,6},{6,2},{2,0},{1,5},{5,9},... | collective-permute-start | bytes 786440 | tf_op jit(solution)/shard_map/ppermute | solution.py:55
  146.1 2.0 %hop_add.14 = (bf16[128,1024]{1,0:T(8,128)(2,1)}, bf16[128,1024]{1,0:T(8,128)(2,1)}) custom-call(bf16[512,2048]{1,0:T(8,128)(2,1)S(1)} %down_mix.6.rest_0_.refs_0_.refs_2_.refs_1_.refs_5_.refs_6_, bf16[512,2048]{1,0:T(8,128)(2,1)S(1)} %down_mix.6.rest_0_.refs_0_.refs_2_.refs_1_.refs_5_.refs_6_, ...), custom_call_target="tpu_custom_call" | custom-call | flops 1000000000 | bytes 2621440 | tf_op jit(solution)/shard_map/hop_add/pallas_call | solution.py:305
  148.1 3.1 %collective-permute-start.31 = (bf16[128,1024]{1,0:T(8,128)(2,1)}, bf16[128,1024]{1,0:T(8,128)(2,1)S(1)}, u32[]{:S(2)}, u32[]{:S(2)}) collective-permute-start(bf16[128,1024]{1,0:T(8,128)(2,1)} %get-tuple-element.38), channel_id=1, source_target_pairs={{0,4},{4,8},{8,12},{12,14},{14,10},{10,6},{6,2},{2,0},{1,5},{5,9},... | collective-permute-start | bytes 786440 | tf_op jit(solution)/shard_map/ppermute | solution.py:55
  155.6 2.4 %collective-permute-start.25 = (bf16[128,1024]{1,0:T(8,128)(2,1)S(1)}, bf16[128,1024]{1,0:T(8,128)(2,1)S(1)}, u32[]{:S(2)}, u32[]{:S(2)}) collective-permute-start(bf16[128,1024]{1,0:T(8,128)(2,1)S(1)} %get-tuple-element.32), channel_id=1, source_target_pairs={{0,4},{4,8},{8,12},{12,14},{14,10},{10,6},{6,2},{2,0},{1,5},{5,9},... | collective-permute-start | bytes 786440 | tf_op jit(solution)/shard_map/ppermute | solution.py:55
  159.9 2.1 %collective-permute-start.33 = (bf16[128,1024]{1,0:T(8,128)(2,1)S(1)}, bf16[128,1024]{1,0:T(8,128)(2,1)S(1)}, u32[]{:S(2)}, u32[]{:S(2)}) collective-permute-start(bf16[128,1024]{1,0:T(8,128)(2,1)S(1)} %get-tuple-element.40), channel_id=1, source_target_pairs={{0,4},{4,8},{8,12},{12,14},{14,10},{10,6},{6,2},{2,0},{1,5},{5,9},... | collective-permute-start | bytes 786440 | tf_op jit(solution)/shard_map/ppermute | solution.py:55
  164.5 2.2 %collective-permute-done.26.refs_1_ = bf16[128,1024]{1,0:T(8,128)(2,1)S(1)} collective-permute-done((bf16[128,1024]{1,0:T(8,128)(2,1)S(1)}, bf16[128,1024]{1,0:T(8,128)(2,1)S(1)}, u32[]{:S(2)}, u32[]{:S(2)}) %collective-permute-start.26) | collective-permute-done | bytes 262176 | tf_op jit(solution)/shard_map/ppermute | solution.py:58
  167.3 2.2 %collective-permute-done.34.refs_3_ = bf16[128,1024]{1,0:T(8,128)(2,1)S(1)} collective-permute-done((bf16[128,1024]{1,0:T(8,128)(2,1)S(1)}, bf16[128,1024]{1,0:T(8,128)(2,1)S(1)}, u32[]{:S(2)}, u32[]{:S(2)}) %collective-permute-start.34) | collective-permute-done | bytes 262176 | tf_op jit(solution)/shard_map/ppermute | solution.py:58
  169.5 2.1 %last_add.1 = bf16[128,2048]{1,0:T(8,128)(2,1)} custom-call(bf16[512,2048]{1,0:T(8,128)(2,1)S(1)} %copy-done.1, bf16[512,2048]{1,0:T(8,128)(2,1)S(1)} %copy-done.1, bf16[512,2048]{1,0:T(8,128)(2,1)} %collective-permute-done.17.refs_7_.refs_8_.refs_2_.refs_3_.taken_0.taken_1, ...), custom_call_target="tpu_custom_call" | custom-call | tf_op jit(solution)/shard_map/last_add/pallas_call | solution.py:337
  (121 shorter events, 45.1 us)
Async XLA Ops:
  3.7 15.5 %collective-permute-start = (bf16[64,4224]{1,0:T(8,128)(2,1)}, bf16[64,4224]{1,0:T(8,128)(2,1)S(1)}, u32[]{:S(2)}, u32[]{:S(2)}) collective-permute-start(bf16[64,4224]{1,0:T(8,128)(2,1)} %prep.1.refs_0_), channel_id=1, source_target_pairs={{0,4},{4,8},{8,12},{12,14},{14,10},{10,6},{6,2},{2,0},{1,5},{5,9},... | collective-permute-start | bytes 1622024 | tf_op jit(solution)/shard_map/ppermute | solution.py:55
  6.7 14.2 %collective-permute-start.1 = (bf16[64,4224]{1,0:T(8,128)(2,1)}, bf16[64,4224]{1,0:T(8,128)(2,1)S(1)}, u32[]{:S(2)}, u32[]{:S(2)}) collective-permute-start(bf16[64,4224]{1,0:T(8,128)(2,1)} %prep.1.refs_0_), channel_id=1, source_target_pairs={{4,0},{8,4},{12,8},{14,12},{10,14},{6,10},{2,6},{0,2},{5,1},{9,5},... | collective-permute-start | bytes 1622024 | tf_op jit(solution)/shard_map/ppermute | solution.py:58
  19.1 13.4 %collective-permute-start.2 = (bf16[64,4224]{1,0:T(8,128)(2,1)S(1)}, bf16[64,4224]{1,0:T(8,128)(2,1)S(1)}, u32[]{:S(2)}, u32[]{:S(2)}) collective-permute-start(bf16[64,4224]{1,0:T(8,128)(2,1)S(1)} %collective-permute-done.refs_1_), channel_id=1, source_target_pairs={{0,4},{4,8},{8,12},{12,14},{14,10},{10,6},{6,2},{2,0},{1,5},{5,9},... | collective-permute-start | bytes 1622024 | tf_op jit(solution)/shard_map/ppermute | solution.py:55
  20.9 15.6 %collective-permute-start.7 = (bf16[64,4224]{1,0:T(8,128)(2,1)S(1)}, bf16[64,4224]{1,0:T(8,128)(2,1)S(1)}, u32[]{:S(2)}, u32[]{:S(2)}) collective-permute-start(bf16[64,4224]{1,0:T(8,128)(2,1)S(1)} %collective-permute-done.1.refs_2_), channel_id=1, source_target_pairs={{4,0},{8,4},{12,8},{14,12},{10,14},{6,10},{2,6},{0,2},{5,1},{9,5},... | collective-permute-start | bytes 1622024 | tf_op jit(solution)/shard_map/ppermute | solution.py:58
  32.6 12.6 %collective-permute-start.8 = (bf16[64,4224]{1,0:T(8,128)(2,1)S(1)}, bf16[64,4224]{1,0:T(8,128)(2,1)S(1)}, u32[]{:S(2)}, u32[]{:S(2)}) collective-permute-start(bf16[64,4224]{1,0:T(8,128)(2,1)S(1)} %collective-permute-done.2.refs_3_), channel_id=1, source_target_pairs={{0,4},{4,8},{8,12},{12,14},{14,10},{10,6},{6,2},{2,0},{1,5},{5,9},... | collective-permute-start | bytes 1622024 | tf_op jit(solution)/shard_map/ppermute | solution.py:55
  34.1 22.8 %collective-permute-start.3 = (bf16[64,4224]{1,0:T(8,128)(2,1)}, bf16[64,4224]{1,0:T(8,128)(2,1)S(1)}, u32[]{:S(2)}, u32[]{:S(2)}) collective-permute-start(bf16[64,4224]{1,0:T(8,128)(2,1)} %prep.1.refs_0_), channel_id=1, source_target_pairs={{0,1},{1,0},{2,3},{3,2},{4,5},{5,4},{6,7},{7,6},{8,9},{9,8},{10,11... | collective-permute-start | bytes 1622024 | tf_op jit(solution)/shard_map/ppermute | solution.py:62
  35.9 22.8 %collective-permute-start.4 = (bf16[64,4224]{1,0:T(8,128)(2,1)S(1)}, bf16[64,4224]{1,0:T(8,128)(2,1)S(1)}, u32[]{:S(2)}, u32[]{:S(2)}) collective-permute-start(bf16[64,4224]{1,0:T(8,128)(2,1)S(1)} %collective-permute-done.refs_1_), channel_id=1, source_target_pairs={{0,1},{1,0},{2,3},{3,2},{4,5},{5,4},{6,7},{7,6},{8,9},{9,8},{10,11... | collective-permute-start | bytes 1622024 | tf_op jit(solution)/shard_map/ppermute | solution.py:62
  36.5 23.3 %collective-permute-start.5 = (bf16[64,4224]{1,0:T(8,128)(2,1)S(1)}, bf16[64,4224]{1,0:T(8,128)(2,1)S(1)}, u32[]{:S(2)}, u32[]{:S(2)}) collective-permute-start(bf16[64,4224]{1,0:T(8,128)(2,1)S(1)} %collective-permute-done.1.refs_2_), channel_id=1, source_target_pairs={{0,1},{1,0},{2,3},{3,2},{4,5},{5,4},{6,7},{7,6},{8,9},{9,8},{10,11... | collective-permute-start | bytes 1622024 | tf_op jit(solution)/shard_map/ppermute | solution.py:62
  36.5 23.2 %collective-permute-start.6 = (bf16[64,4224]{1,0:T(8,128)(2,1)S(1)}, bf16[64,4224]{1,0:T(8,128)(2,1)S(1)}, u32[]{:S(2)}, u32[]{:S(2)}) collective-permute-start(bf16[64,4224]{1,0:T(8,128)(2,1)S(1)} %collective-permute-done.2.refs_3_), channel_id=1, source_target_pairs={{0,1},{1,0},{2,3},{3,2},{4,5},{5,4},{6,7},{7,6},{8,9},{9,8},{10,11... | collective-permute-start | bytes 1622024 | tf_op jit(solution)/shard_map/ppermute | solution.py:62
  45.2 11.7 %collective-permute-start.9 = (bf16[64,4224]{1,0:T(8,128)(2,1)S(1)}, bf16[64,4224]{1,0:T(8,128)(2,1)S(1)}, u32[]{:S(2)}, u32[]{:S(2)}) collective-permute-start(bf16[64,4224]{1,0:T(8,128)(2,1)S(1)} %collective-permute-done.7.refs_0_), channel_id=1, source_target_pairs={{4,0},{8,4},{12,8},{14,12},{10,14},{6,10},{2,6},{0,2},{5,1},{9,5},... | collective-permute-start | bytes 1622024 | tf_op jit(solution)/shard_map/ppermute | solution.py:58
  56.9 25.8 %collective-permute-start.12 = (bf16[64,4224]{1,0:T(8,128)(2,1)S(1)}, bf16[64,4224]{1,0:T(8,128)(2,1)S(1)}, u32[]{:S(2)}, u32[]{:S(2)}) collective-permute-start(bf16[64,4224]{1,0:T(8,128)(2,1)S(1)} %collective-permute-done.7.refs_0_), channel_id=1, source_target_pairs={{0,1},{1,0},{2,3},{3,2},{4,5},{5,4},{6,7},{7,6},{8,9},{9,8},{10,11... | collective-permute-start | bytes 1622024 | tf_op jit(solution)/shard_map/ppermute | solution.py:62
  57.7 18.1 %collective-permute-start.10 = (bf16[32,4224]{1,0:T(8,128)(2,1)S(1)}, bf16[32,4224]{1,0:T(8,128)(2,1)S(1)}, u32[]{:S(2)}, u32[]{:S(2)}) collective-permute-start(bf16[32,4224]{1,0:T(8,128)(2,1)S(1)} %slice.24), channel_id=1, source_target_pairs={{0,4},{4,8},{8,12},{12,14},{14,10},{10,6},{6,2},{2,0},{1,5},{5,9},... | collective-permute-start | bytes 811016 | tf_op jit(solution)/shard_map/ppermute | solution.py:55
  58.7 17.3 %collective-permute-start.11 = (bf16[32,4224]{1,0:T(8,128)(2,1)S(1)}, bf16[32,4224]{1,0:T(8,128)(2,1)S(1)}, u32[]{:S(2)}, u32[]{:S(2)}) collective-permute-start(bf16[32,4224]{1,0:T(8,128)(2,1)S(1)} %slice.25), channel_id=1, source_target_pairs={{4,0},{8,4},{12,8},{14,12},{10,14},{6,10},{2,6},{0,2},{5,1},{9,5},... | collective-permute-start | bytes 811016 | tf_op jit(solution)/shard_map/ppermute | solution.py:58
  59.8 22.9 %collective-permute-start.13 = (bf16[64,4224]{1,0:T(8,128)(2,1)S(1)}, bf16[64,4224]{1,0:T(8,128)(2,1)S(1)}, u32[]{:S(2)}, u32[]{:S(2)}) collective-permute-start(bf16[64,4224]{1,0:T(8,128)(2,1)S(1)} %collective-permute-done.8.refs_1_), channel_id=1, source_target_pairs={{0,1},{1,0},{2,3},{3,2},{4,5},{5,4},{6,7},{7,6},{8,9},{9,8},{10,11... | collective-permute-start | bytes 1622024 | tf_op jit(solution)/shard_map/ppermute | solution.py:62
  59.8 22.9 %collective-permute-start.14 = (bf16[64,4224]{1,0:T(8,128)(2,1)S(1)}, bf16[64,4224]{1,0:T(8,128)(2,1)S(1)}, u32[]{:S(2)}, u32[]{:S(2)}) collective-permute-start(bf16[64,4224]{1,0:T(8,128)(2,1)S(1)} %collective-permute-done.9.refs_2_), channel_id=1, source_target_pairs={{0,1},{1,0},{2,3},{3,2},{4,5},{5,4},{6,7},{7,6},{8,9},{9,8},{10,11... | collective-permute-start | bytes 1622024 | tf_op jit(solution)/shard_map/ppermute | solution.py:62
  102.8 37.1 %collective-permute-start.17 = (bf16[512,2048]{1,0:T(8,128)(2,1)}, bf16[512,2048]{1,0:T(8,128)(2,1)}, u32[]{:S(2)}, u32[]{:S(2)}) collective-permute-start(bf16[512,2048]{1,0:T(8,128)(2,1)} %down_mix.4.rest_0_), channel_id=1, source_target_pairs={{0,1},{1,0},{2,3},{3,2},{4,5},{5,4},{6,7},{7,6},{8,9},{9,8},{10,11... | collective-permute-start | bytes 6291464 | tf_op jit(solution)/shard_map/ppermute | solution.py:62
  114.0 13.7 %collective-permute-start.19 = (bf16[64,1024]{1,0:T(8,128)(2,1)}, bf16[64,1024]{1,0:T(8,128)(2,1)}, u32[]{:S(2)}, u32[]{:S(2)}) collective-permute-start(bf16[64,1024]{1,0:T(8,128)(2,1)} %get-tuple-element.26), channel_id=1, source_target_pairs={{0,4},{4,8},{8,12},{12,14},{14,10},{10,6},{6,2},{2,0},{1,5},{5,9},... | collective-permute-start | bytes 393224 | tf_op jit(solution)/shard_map/ppermute | solution.py:55
  114.9 12.8 %collective-permute-start.20 = (bf16[64,1024]{1,0:T(8,128)(2,1)}, bf16[64,1024]{1,0:T(8,128)(2,1)}, u32[]{:S(2)}, u32[]{:S(2)}) collective-permute-start(bf16[64,1024]{1,0:T(8,128)(2,1)} %get-tuple-element.27), channel_id=1, source_target_pairs={{4,0},{8,4},{12,8},{14,12},{10,14},{6,10},{2,6},{0,2},{5,1},{9,5},... | collective-permute-start | bytes 393224 | tf_op jit(solution)/shard_map/ppermute | solution.py:58
  117.7 13.5 %collective-permute-start.27 = (bf16[64,1024]{1,0:T(8,128)(2,1)}, bf16[64,1024]{1,0:T(8,128)(2,1)S(1)}, u32[]{:S(2)}, u32[]{:S(2)}) collective-permute-start(bf16[64,1024]{1,0:T(8,128)(2,1)} %get-tuple-element.34), channel_id=1, source_target_pairs={{0,4},{4,8},{8,12},{12,14},{14,10},{10,6},{6,2},{2,0},{1,5},{5,9},... | collective-permute-start | bytes 393224 | tf_op jit(solution)/shard_map/ppermute | solution.py:55
  118.7 12.6 %collective-permute-start.28 = (bf16[64,1024]{1,0:T(8,128)(2,1)}, bf16[64,1024]{1,0:T(8,128)(2,1)S(1)}, u32[]{:S(2)}, u32[]{:S(2)}) collective-permute-start(bf16[64,1024]{1,0:T(8,128)(2,1)} %get-tuple-element.35), channel_id=1, source_target_pairs={{4,0},{8,4},{12,8},{14,12},{10,14},{6,10},{2,6},{0,2},{5,1},{9,5},... | collective-permute-start | bytes 393224 | tf_op jit(solution)/shard_map/ppermute | solution.py:58
  122.5 28.7 %all-to-all-start = ((bf16[8,2,8320]{2,1,0:T(2,128)(2,1)}), bf16[8,2,8320]{2,1,0:T(2,128)(2,1)}, u32[]{:S(2)}, u32[]{:S(2)}) async-start(bf16[8,2,8320]{2,1,0:T(2,128)(2,1)} %reshape.171), calls=%async_computation | async-start | bytes 532480 | tf_op jit(solution)/shard_map/all_to_all | solution.py:409
  129.1 10.9 %collective-permute-start.21 = (bf16[128,1024]{1,0:T(8,128)(2,1)S(1)}, bf16[128,1024]{1,0:T(8,128)(2,1)S(1)}, u32[]{:S(2)}, u32[]{:S(2)}) collective-permute-start(bf16[128,1024]{1,0:T(8,128)(2,1)S(1)} %get-tuple-element.28), channel_id=1, source_target_pairs={{0,4},{4,8},{8,12},{12,14},{14,10},{10,6},{6,2},{2,0},{1,5},{5,9},... | collective-permute-start | bytes 786440 | tf_op jit(solution)/shard_map/ppermute | solution.py:55
  132.5 13.0 %collective-permute-start.29 = (bf16[128,1024]{1,0:T(8,128)(2,1)S(1)}, bf16[128,1024]{1,0:T(8,128)(2,1)S(1)}, u32[]{:S(2)}, u32[]{:S(2)}) collective-permute-start(bf16[128,1024]{1,0:T(8,128)(2,1)S(1)} %get-tuple-element.36), channel_id=1, source_target_pairs={{0,4},{4,8},{8,12},{12,14},{14,10},{10,6},{6,2},{2,0},{1,5},{5,9},... | collective-permute-start | bytes 786440 | tf_op jit(solution)/shard_map/ppermute | solution.py:55
  134.5 11.6 %collective-permute-start.30 = (bf16[128,1024]{1,0:T(8,128)(2,1)S(1)}, bf16[128,1024]{1,0:T(8,128)(2,1)S(1)}, u32[]{:S(2)}, u32[]{:S(2)}) collective-permute-start(bf16[128,1024]{1,0:T(8,128)(2,1)S(1)} %get-tuple-element.37), channel_id=1, source_target_pairs={{4,0},{8,4},{12,8},{14,12},{10,14},{6,10},{2,6},{0,2},{5,1},{9,5},... | collective-permute-start | bytes 786440 | tf_op jit(solution)/shard_map/ppermute | solution.py:58
  (26 other events, 165.8 us)
